TPU v7x, 32 devices: a whole 2x2x4 slice. The times are simulated.
32 devices in a mesh: fsdp: 16 (over z, y, core), dp: 2 (over x).
Axes of the slice: x: 2, y: 2, z: 4, core: 2. Of those that a mesh axis runs over, the one named last changes fastest.
Arguments:
- block_input: bfloat16 [160, 416, 768], P(('fsdp', 'dp')), may hold values from -6 to 6
- segment_ids: int32 [160, 416], P(('fsdp', 'dp')), may hold values from -1 to 24, as said below
- ln1_gain: bfloat16 [768], P('fsdp'), may hold values from 0.099609375 to 1.8984375
- ln1_bias: bfloat16 [768], P('fsdp'), may hold values from -3 to 3
- qkv_weight: bfloat16 [768, 2304], P('fsdp'), may hold values from -0.21875 to 0.21875
- qv_bias: bfloat16 [1536], P('fsdp'), may hold values from -3 to 3
- out_weight: bfloat16 [768, 768], P('fsdp'), may hold values from -0.875 to 0.875
- out_bias: bfloat16 [768], P('fsdp'), may hold values from -3 to 3
- ln2_gain: bfloat16 [768], P('fsdp'), may hold values from 0.099609375 to 1.8984375
- ln2_bias: bfloat16 [768], P('fsdp'), may hold values from -3 to 3
- up_weight: bfloat16 [768, 3072], P('fsdp'), may hold values from -0.21875 to 0.21875
- up_bias: bfloat16 [3072], P('fsdp'), may hold values from -3 to 3
- down_weight: bfloat16 [3072, 768], P('fsdp'), may hold values from -0.109375 to 0.109375
- down_bias: bfloat16 [768], P('fsdp'), may hold values from -3 to 3
- out_cotangent: bfloat16 [160, 416, 768], P(('fsdp', 'dp')), may hold values from -6 to 6
Outputs:
- block_output: bfloat16 [160, 416, 768], P(('fsdp', 'dp'))
- input_grad: bfloat16 [160, 416, 768], P(('fsdp', 'dp'))
- ln1_gain_grad: float32 [768], P('fsdp')
- ln1_bias_grad: float32 [768], P('fsdp')
- qkv_weight_grad: float32 [768, 2304], P('fsdp')
- qv_bias_grad: float32 [1536], P('fsdp')
- out_weight_grad: float32 [768, 768], P('fsdp')
- out_bias_grad: float32 [768], P('fsdp')
- ln2_gain_grad: float32 [768], P('fsdp')
- ln2_bias_grad: float32 [768], P('fsdp')
- up_weight_grad: float32 [768, 3072], P('fsdp')
- up_bias_grad: float32 [3072], P('fsdp')
- down_weight_grad: float32 [3072, 768], P('fsdp')
- down_bias_grad: float32 [768], P('fsdp')
Inputs may be any that keep to these rules, and one draw needn't show every extreme that they name: `segment_ids`: each packed row holds whole images of h x w slots with h and w from 4 to 14, numbered 0, 1, 2 in order from the row's start, followed by padding slots marked -1 (at least one in every row); some row holds the most images that fit.
All inputs are finite; a program needn't handle non-finite values.
Results may differ from a plain program's by a relative error of at most 0.013.
Values may be sent and summed in bfloat16 or wider, within the bound.
A program may use at most 256 MiB of HBM per device.

v0:
```python
import jax
import jax.numpy as jnp
from jax import lax
from jax.sharding import PartitionSpec as P

HEAD_DIM = 64


def layer_norm(values, gain, shift):
    center = values - jnp.mean(values, axis=-1, keepdims=True)
    spread = jnp.mean(center * center, axis=-1, keepdims=True)
    return center * lax.rsqrt(spread + 1e-06) * gain + shift


def gelu_exact(values):
    return jax.nn.gelu(values, approximate=False)


def masked_scores(queries, keys_row, segment_row):
    scores = (
        jnp.einsum("qhe,khe->hqk", queries, keys_row, preferred_element_type=jnp.float32) * 0.125
    )
    allowed = segment_row[:, None] == segment_row[None, :]
    return jnp.where(allowed[None], scores, -jnp.inf)


def row_forward(items):
    queries, keys_row, values_row, segment_row = items
    scores = masked_scores(queries, keys_row, segment_row)
    highest = jnp.max(scores, axis=-1, keepdims=True)
    expo = jnp.exp(scores - highest)
    totals = jnp.sum(expo, axis=-1, keepdims=True)
    probs = (expo / totals).astype(jnp.bfloat16)
    mixed = jnp.einsum("hqk,khe->qhe", probs, values_row, preferred_element_type=jnp.float32)
    return (mixed.astype(jnp.bfloat16), (highest + jnp.log(totals))[..., 0])


def row_backward(items):
    queries, keys_row, values_row, segment_row, grad_mixed, logsum = items
    scores = masked_scores(queries, keys_row, segment_row)
    probs = jnp.exp(scores - logsum[..., None])
    grad_probs = jnp.einsum(
        "qhe,khe->hqk", grad_mixed, values_row, preferred_element_type=jnp.float32
    )
    grad_values = jnp.einsum(
        "hqk,qhe->khe", probs.astype(jnp.bfloat16), grad_mixed, preferred_element_type=jnp.float32
    ).astype(jnp.bfloat16)
    inner = jnp.sum(probs * grad_probs, axis=-1, keepdims=True)
    grad_scores = (probs * (grad_probs - inner)).astype(jnp.bfloat16)
    grad_queries = (
        jnp.einsum("hqk,khe->qhe", grad_scores, keys_row, preferred_element_type=jnp.float32)
        * 0.125
    ).astype(jnp.bfloat16)
    grad_keys = (
        jnp.einsum("hqk,qhe->khe", grad_scores, queries, preferred_element_type=jnp.float32) * 0.125
    ).astype(jnp.bfloat16)
    return (grad_queries, grad_keys, grad_values)


def per_device(
    block_input,
    segment_ids,
    ln1_gain,
    ln1_bias,
    qkv_weight,
    qv_bias,
    out_weight,
    out_bias,
    ln2_gain,
    ln2_bias,
    up_weight,
    up_bias,
    down_weight,
    down_bias,
    out_cotangent,
):
    rows, slots, width = block_input.shape
    heads = width // HEAD_DIM
    shape_four = (rows, slots, heads, HEAD_DIM)
    attn_shards = (ln1_gain, ln1_bias, qkv_weight, qv_bias, out_weight, out_bias)
    mlp_shards = (ln2_gain, ln2_bias, up_weight, up_bias, down_weight, down_bias)
    attn_full = (
        lax.all_gather(attn_shards[0], "fsdp", axis=0, tiled=True),
        lax.all_gather(attn_shards[1], "fsdp", axis=0, tiled=True),
        lax.all_gather(attn_shards[2], "fsdp", axis=0, tiled=True),
        lax.all_gather(attn_shards[3], "fsdp", axis=0, tiled=True),
        lax.all_gather(attn_shards[4], "fsdp", axis=0, tiled=True),
        lax.all_gather(attn_shards[5], "fsdp", axis=0, tiled=True),
    )
    gain_one, shift_one, qkv_full, bias_full, proj_full, proj_bias = attn_full
    flat = block_input.reshape(-1, width).astype(jnp.float32)
    normed, norm_back = jax.vjp(
        layer_norm, flat, gain_one.astype(jnp.float32), shift_one.astype(jnp.float32)
    )
    normed_low = normed.astype(jnp.bfloat16)
    projected = jnp.dot(normed_low, qkv_full, preferred_element_type=jnp.float32)
    bias_wide = bias_full.astype(jnp.float32)
    queries = (projected[:, :width] + bias_wide[:width]).astype(jnp.bfloat16).reshape(shape_four)
    keys_all = projected[:, width : 2 * width].astype(jnp.bfloat16).reshape(shape_four)
    values_all = (
        (projected[:, 2 * width :] + bias_wide[width:]).astype(jnp.bfloat16).reshape(shape_four)
    )
    mixed, logsum = lax.map(row_forward, (queries, keys_all, values_all, segment_ids))
    mixed_flat = mixed.reshape(-1, width)
    middle = (
        flat
        + jnp.dot(mixed_flat, proj_full, preferred_element_type=jnp.float32)
        + proj_bias.astype(jnp.float32)
    )
    mlp_full = (
        lax.all_gather(mlp_shards[0], "fsdp", axis=0, tiled=True),
        lax.all_gather(mlp_shards[1], "fsdp", axis=0, tiled=True),
        lax.all_gather(mlp_shards[2], "fsdp", axis=0, tiled=True),
        lax.all_gather(mlp_shards[3], "fsdp", axis=0, tiled=True),
        lax.all_gather(mlp_shards[4], "fsdp", axis=0, tiled=True),
        lax.all_gather(mlp_shards[5], "fsdp", axis=0, tiled=True),
    )
    gain_two, shift_two, up_full, up_shift, down_full, down_shift = mlp_full
    normed_two, norm_two_back = jax.vjp(
        layer_norm, middle, gain_two.astype(jnp.float32), shift_two.astype(jnp.float32)
    )
    normed_two_low = normed_two.astype(jnp.bfloat16)
    hidden_pre = jnp.dot(
        normed_two_low, up_full, preferred_element_type=jnp.float32
    ) + up_shift.astype(jnp.float32)
    hidden_act, gelu_back = jax.vjp(gelu_exact, hidden_pre)
    hidden_low = hidden_act.astype(jnp.bfloat16)
    output = (
        middle
        + jnp.dot(hidden_low, down_full, preferred_element_type=jnp.float32)
        + down_shift.astype(jnp.float32)
    )
    block_output = output.astype(jnp.bfloat16).reshape(rows, slots, width)
    mlp_again = (
        lax.all_gather(mlp_shards[0], "fsdp", axis=0, tiled=True),
        lax.all_gather(mlp_shards[1], "fsdp", axis=0, tiled=True),
        lax.all_gather(mlp_shards[2], "fsdp", axis=0, tiled=True),
        lax.all_gather(mlp_shards[3], "fsdp", axis=0, tiled=True),
        lax.all_gather(mlp_shards[4], "fsdp", axis=0, tiled=True),
        lax.all_gather(mlp_shards[5], "fsdp", axis=0, tiled=True),
    )
    up_back = mlp_again[2]
    down_back = mlp_again[4]
    cotangent = out_cotangent.reshape(-1, width)
    cot_wide = cotangent.astype(jnp.float32)
    down_bias_grad = jnp.sum(cot_wide, axis=0)
    down_weight_grad = jnp.einsum(
        "nf,nd->fd", hidden_low, cotangent, preferred_element_type=jnp.float32
    )
    grad_hidden = jnp.einsum("nd,fd->nf", cotangent, down_back, preferred_element_type=jnp.float32)
    grad_pre = gelu_back(grad_hidden)[0].astype(jnp.bfloat16)
    up_bias_grad = jnp.sum(grad_pre.astype(jnp.float32), axis=0)
    up_weight_grad = jnp.einsum(
        "nd,nf->df", normed_two_low, grad_pre, preferred_element_type=jnp.float32
    )
    grad_normed_two = jnp.einsum("nf,df->nd", grad_pre, up_back, preferred_element_type=jnp.float32)
    grad_mid_norm, gain_two_grad, shift_two_grad = norm_two_back(grad_normed_two)
    grad_middle = cot_wide + grad_mid_norm
    mlp_local = (
        gain_two_grad,
        shift_two_grad,
        up_weight_grad,
        up_bias_grad,
        down_weight_grad,
        down_bias_grad,
    )
    mlp_owned = (
        lax.psum_scatter(mlp_local[0], "fsdp", scatter_dimension=0, tiled=True),
        lax.psum_scatter(mlp_local[1], "fsdp", scatter_dimension=0, tiled=True),
        lax.psum_scatter(mlp_local[2], "fsdp", scatter_dimension=0, tiled=True),
        lax.psum_scatter(mlp_local[3], "fsdp", scatter_dimension=0, tiled=True),
        lax.psum_scatter(mlp_local[4], "fsdp", scatter_dimension=0, tiled=True),
        lax.psum_scatter(mlp_local[5], "fsdp", scatter_dimension=0, tiled=True),
    )
    mlp_summed = (
        lax.psum(mlp_owned[0].astype(jnp.bfloat16), "dp").astype(jnp.float32),
        lax.psum(mlp_owned[1].astype(jnp.bfloat16), "dp").astype(jnp.float32),
        lax.psum(mlp_owned[2].astype(jnp.bfloat16), "dp").astype(jnp.float32),
        lax.psum(mlp_owned[3].astype(jnp.bfloat16), "dp").astype(jnp.float32),
        lax.psum(mlp_owned[4].astype(jnp.bfloat16), "dp").astype(jnp.float32),
        lax.psum(mlp_owned[5].astype(jnp.bfloat16), "dp").astype(jnp.float32),
    )
    attn_again = (
        lax.all_gather(attn_shards[0], "fsdp", axis=0, tiled=True),
        lax.all_gather(attn_shards[1], "fsdp", axis=0, tiled=True),
        lax.all_gather(attn_shards[2], "fsdp", axis=0, tiled=True),
        lax.all_gather(attn_shards[3], "fsdp", axis=0, tiled=True),
        lax.all_gather(attn_shards[4], "fsdp", axis=0, tiled=True),
        lax.all_gather(attn_shards[5], "fsdp", axis=0, tiled=True),
    )
    qkv_back = attn_again[2]
    proj_back = attn_again[4]
    grad_branch = grad_middle.astype(jnp.bfloat16)
    out_bias_grad = jnp.sum(grad_branch.astype(jnp.float32), axis=0)
    out_weight_grad = jnp.einsum(
        "nd,ne->de", mixed_flat, grad_branch, preferred_element_type=jnp.float32
    )
    grad_mixed = jnp.einsum(
        "ne,de->nd", grad_branch, proj_back, preferred_element_type=jnp.float32
    ).astype(jnp.bfloat16)
    grad_queries, grad_keys, grad_values = lax.map(
        row_backward,
        (queries, keys_all, values_all, segment_ids, grad_mixed.reshape(shape_four), logsum),
    )
    grad_queries = grad_queries.reshape(-1, width)
    grad_keys = grad_keys.reshape(-1, width)
    grad_values = grad_values.reshape(-1, width)
    grad_projected = jnp.concatenate([grad_queries, grad_keys, grad_values], axis=1)
    qv_bias_grad = jnp.concatenate(
        [
            jnp.sum(grad_queries.astype(jnp.float32), axis=0),
            jnp.sum(grad_values.astype(jnp.float32), axis=0),
        ]
    )
    qkv_weight_grad = jnp.einsum(
        "nd,nc->dc", normed_low, grad_projected, preferred_element_type=jnp.float32
    )
    grad_normed = jnp.einsum(
        "nc,dc->nd", grad_projected, qkv_back, preferred_element_type=jnp.float32
    )
    grad_flat_norm, gain_one_grad, shift_one_grad = norm_back(grad_normed)
    input_grad = (grad_middle + grad_flat_norm).astype(jnp.bfloat16).reshape(rows, slots, width)
    attn_local = (
        gain_one_grad,
        shift_one_grad,
        qkv_weight_grad,
        qv_bias_grad,
        out_weight_grad,
        out_bias_grad,
    )
    attn_owned = (
        lax.psum_scatter(attn_local[0], "fsdp", scatter_dimension=0, tiled=True),
        lax.psum_scatter(attn_local[1], "fsdp", scatter_dimension=0, tiled=True),
        lax.psum_scatter(attn_local[2], "fsdp", scatter_dimension=0, tiled=True),
        lax.psum_scatter(attn_local[3], "fsdp", scatter_dimension=0, tiled=True),
        lax.psum_scatter(attn_local[4], "fsdp", scatter_dimension=0, tiled=True),
        lax.psum_scatter(attn_local[5], "fsdp", scatter_dimension=0, tiled=True),
    )
    attn_summed = (
        lax.psum(attn_owned[0].astype(jnp.bfloat16), "dp").astype(jnp.float32),
        lax.psum(attn_owned[1].astype(jnp.bfloat16), "dp").astype(jnp.float32),
        lax.psum(attn_owned[2].astype(jnp.bfloat16), "dp").astype(jnp.float32),
        lax.psum(attn_owned[3].astype(jnp.bfloat16), "dp").astype(jnp.float32),
        lax.psum(attn_owned[4].astype(jnp.bfloat16), "dp").astype(jnp.float32),
        lax.psum(attn_owned[5].astype(jnp.bfloat16), "dp").astype(jnp.float32),
    )
    return (
        block_output,
        input_grad,
        attn_summed[0],
        attn_summed[1],
        attn_summed[2],
        attn_summed[3],
        attn_summed[4],
        attn_summed[5],
        mlp_summed[0],
        mlp_summed[1],
        mlp_summed[2],
        mlp_summed[3],
        mlp_summed[4],
        mlp_summed[5],
    )


def solution(mesh):
    return jax.shard_map(
        per_device,
        mesh=mesh,
        in_specs=(
            P(("fsdp", "dp"), None, None),
            P(("fsdp", "dp"), None),
            P("fsdp"),
            P("fsdp"),
            P("fsdp", None),
            P("fsdp"),
            P("fsdp", None),
            P("fsdp"),
            P("fsdp"),
            P("fsdp"),
            P("fsdp", None),
            P("fsdp"),
            P("fsdp", None),
            P("fsdp"),
            P(("fsdp", "dp"), None, None),
        ),
        out_specs=(
            P(("fsdp", "dp"), None, None),
            P(("fsdp", "dp"), None, None),
            P("fsdp"),
            P("fsdp"),
            P("fsdp", None),
            P("fsdp"),
            P("fsdp", None),
            P("fsdp"),
            P("fsdp"),
            P("fsdp"),
            P("fsdp", None),
            P("fsdp"),
            P("fsdp", None),
            P("fsdp"),
        ),
        check_vma=False,
    )
```

profile of v0, /device:TPU:0, one launch (start us, length us, event | category | flops | bytes accessed | tf_op | source)
XLA Modules:
  0.0 992.4 jit_solution(8717277212317786385)
XLA Ops:
  20.1 64.0 %all-reduce.17 = (bf16[768]{0:T(1024)(128)(2,1)S(1)}, bf16[768]{0:T(1024)(128)(2,1)S(1)}, bf16[1536]{0:T(1024)(128)(2,1)S(1)}, bf16[768]{0:T(1024)(128)(2,1)S(1)...) all-reduce(bf16[768]{0:T(1024)(128)(2,1)S(1)} %dynamic-update-slice, ...), channel_id=1, replica_groups=mesh['fsdp'=16,'dp'=2] {'fsdp'}, use_global_device_ids=true, to_apply=%add.1 | all-reduce | flops 9216 | bytes 36864
  86.7 5.0 bitcast_subtract_fusion
  91.7 10.9 %fusion.78 = f32[2080,2304]{1,0:T(8,128)S(1)} fusion(bf16[2080,768]{1,0:T(8,128)(2,1)} %get-tuple-element.243, bf16[768,2304]{1,0:T(8,128)(2,1)} %all-gather.5.cloned.1.call-done), kind=kOutput, calls=%fused_computation.139 | convolution fusion | flops 7361003520 | bytes 25903104 | tf_op jit(solution)/shard_map/dot_general | solution.py:96
  107.0 10.8 %reshape.303 = bf16[5,416,12,64]{3,2,1,0:T(8,128)(2,1)} reshape(bf16[2080,768]{1,0:T(8,128)(2,1)} %get-tuple-element.241) | data formatting | bytes 6389760 | tf_op jit(solution)/shard_map/reshape | solution.py:101
  117.8 10.7 %copy.66 = bf16[5,416,12,64]{1,3,2,0:T(8,128)(2,1)} copy(bf16[5,416,12,64]{3,2,1,0:T(8,128)(2,1)} %reshape.303) | data formatting | bytes 6389760 | tf_op jit(solution)/shard_map/while | solution.py:103
  128.4 7.7 reshape.304
  136.1 10.8 %copy.67 = bf16[5,416,12,64]{1,3,2,0:T(8,128)(2,1)} copy(bf16[5,416,12,64]{3,2,1,0:T(8,128)(2,1)} %reshape.304) | data formatting | bytes 6389760 | tf_op jit(solution)/shard_map/while | solution.py:103
  147.0 8.1 reshape.305
  155.1 10.7 %copy.68 = bf16[5,416,12,64]{1,3,2,0:T(8,128)(2,1)} copy(bf16[5,416,12,64]{3,2,1,0:T(8,128)(2,1)} %reshape.305) | data formatting | bytes 6389760 | tf_op jit(solution)/shard_map/while | solution.py:103
  168.1 59.9 %while.26 = (s32[]{:T(128)}, bf16[5,416,12,64]{1,3,2,0:T(8,128)(2,1)}, f32[5,12,416]{2,1,0:T(8,128)}, bf16[5,416,12,64]{1,3,2,0:T(8,128)(2,1)}, s32[5,416]{1,0:T...) while((s32[]{:T(128)}, bf16[5,416,12,64]{1,3,2,0:T(8,128)(2,1)}, ...), condition=%wide.region_5.6_spmd, body=%wide.region_2.5_spmd.sunk | while | flops 557035648 | bytes 28938200 | solution.py:103
  175.1 5.0 fusion.126
  187.1 4.9 fusion.126
  199.0 5.0 fusion.126
  211.1 4.9 fusion.126
  223.0 5.0 fusion.126
  228.0 7.7 copy.69
  235.7 9.7 reshape.245
  245.4 7.7 fusion.67
  256.3 3.7 multiply_reduce_fusion.5
  260.6 71.5 %multiply_convert_fusion.3 = (bf16[2080,3072]{1,0:T(8,128)(2,1)}, f32[2080,3072]{1,0:T(8,128)}, f32[2080,3072]{1,0:T(8,128)}) fusion(f32[3072]{0:T(1024)S(1)} %copy-done.33, bf16[768,3072]{1,0:T(8,128)(2,1)} %all-gather.9.cloned.1.call-done, f32[2080,768]{1,0:T(8,128)} %fusion.67, f32[768]{0:T(1024)S(1)} %copy-done.35, f32[768]{0:T(1024)S(1)} %copy-done.30, ...), kind=kOutput, calls=%fused_computation.68 | convolution fusion | flops 10244382720 | bytes 75041024 | tf_op jit(solution)/shard_map/dot_general | solution.py:123
  332.1 28.3 %convert_reduce_fusion = (f32[3072]{0:T(1024)}, bf16[2080,3072]{1,0:T(8,128)(2,1)}) fusion(f32[2080,3072]{1,0:T(8,128)} %get-tuple-element.235, bf16[2080,768]{1,0:T(8,128)(2,1)S(1)} %bitcast.159, bf16[3072,768]{1,0:T(8,128)(2,1)} %all-gather.11.cloned.1.call-done, f32[2080,3072]{1,0:T(8,128)} %get-tuple-element.248, f32[3072]{0:T(1024)S(1)} %copy-done.33), kind=kOutput, calls=%fused_computation.66 | convolution fusion | flops 9923294208 | bytes 71835648 | tf_op jit(solution)/shard_map/nd,fd->nf/dot_general | solution.py:150
  360.5 22.1 %multiply_reduce_fusion.1 = (f32[768]{0:T(1024)}, f32[2080]{0:T(1024)S(1)}, f32[768]{0:T(1024)}, f32[2080,768]{1,0:T(8,128)}) fusion(f32[2080,768]{1,0:T(8,128)} %fusion.67, f32[2080]{0:T(1024)S(1)} %fusion.69, f32[2080]{0:T(1024)S(1)} %broadcast_multiply_fusion.1, f32[768]{0:T(1024)S(1)} %copy-done.30, bf16[2080,3072]{1,0:T(8,128)(2,1)} %get-tuple-element.252, ...), kind=kOutput, calls=%fused_computation.98 | convolution fusion | flops 9827446784 | bytes 30311808 | tf_op jit(solution)/shard_map/nf,df->nd/dot_general | solution.py:156
  382.6 4.9 fusion.74
  387.5 5.5 convert_reduce_fusion.5
  393.0 4.3 fusion.80
  397.3 5.3 convolution_convert_fusion
  402.7 10.8 %reshape.294 = bf16[5,416,12,64]{3,2,1,0:T(8,128)(2,1)} reshape(bf16[2080,768]{1,0:T(8,128)(2,1)} %convolution_convert_fusion) | data formatting | bytes 6389760 | tf_op jit(solution)/shard_map/reshape | solution.py:203
  413.5 10.7 %copy.73 = bf16[5,416,12,64]{1,3,2,0:T(8,128)(2,1)} copy(bf16[5,416,12,64]{3,2,1,0:T(8,128)(2,1)} %reshape.294) | data formatting | bytes 6389760 | tf_op jit(solution)/shard_map/while | solution.py:201
  431.4 121.2 %while.27 = (s32[]{:T(128)}, bf16[5,416,12,64]{1,3,2,0:T(8,128)(2,1)}, bf16[5,416,12,64]{1,3,2,0:T(8,128)(2,1)}, bf16[5,416,12,64]{1,3,2,0:T(8,128)(2,1)}, bf16[...) while((s32[]{:T(128)}, ...), condition=%wide.region_12.13_spmd, body=%wide.region_10.12_spmd.sunk | while | flops 1361985664 | bytes 71006704 | solution.py:201
  436.2 5.0 multiply_reduce_fusion.7
  444.4 3.6 fusion.137
  451.1 4.8 fusion.138
  460.4 5.0 multiply_reduce_fusion.7
  468.6 3.6 fusion.137
  475.3 4.7 fusion.138
  484.7 4.9 multiply_reduce_fusion.7
  492.8 3.6 fusion.137
  499.5 4.7 fusion.138
  508.9 4.9 multiply_reduce_fusion.7
  517.0 3.6 fusion.137
  523.7 4.7 fusion.138
  533.0 4.9 multiply_reduce_fusion.7
  541.2 3.6 fusion.137
  547.9 4.7 fusion.138
  552.6 7.7 copy.75
  560.4 8.4 reshape.249
  568.8 7.7 copy.76
  576.5 9.5 reshape.250
  586.0 7.7 copy.77
  593.8 9.5 reshape.251
  606.7 3.8 copy-done.13
  610.5 11.0 %fusion.79 = f32[768,2304]{1,0:T(8,128)} fusion(bf16[2080,768]{1,0:T(8,128)(2,1)S(1)} %copy-done.12, bf16[2080,2304]{0,1:T(8,128)(2,1)S(1)} %constant_dynamic-update-slice_fusion), kind=kOutput, calls=%fused_computation.140 | convolution fusion | flops 7361003520 | bytes 19857408 | tf_op jit(solution)/shard_map/nd,nc->dc/dot_general | solution.py:215
  622.3 19.4 %fusion.70 = f32[768,3072]{1,0:T(8,128)} fusion(bf16[2080,3072]{1,0:T(8,128)(2,1)} %get-tuple-element.252, f32[2080,768]{1,0:T(8,128)} %fusion.67, f32[768]{0:T(1024)S(1)} %copy-done.36, f32[768]{0:T(1024)S(1)} %copy-done.31, f32[2080]{0:T(1024)S(1)} %copy-done.27, f32[2080]{0:T(1024)S(1)} %copy-done.21), kind=kOutput, calls=%fused_computation.133 | convolution fusion | flops 9822658560 | bytes 28629248 | tf_op jit(solution)/shard_map/nd,nf->df/dot_general | solution.py:153
  643.6 15.7 %fusion.81 = f32[3072,768]{1,0:T(8,128)} fusion(bf16[2080,3072]{1,0:T(8,128)(2,1)} %get-tuple-element.234, bf16[2080,768]{1,0:T(8,128)(2,1)S(1)} %bitcast.160), kind=kOutput, calls=%fused_computation.142 | convolution fusion | flops 9814671360 | bytes 25411584 | tf_op jit(solution)/shard_map/nf,nd->fd/dot_general | solution.py:147
  664.1 4.5 convert_reduce_fusion.1
  668.9 19.5 %fusion.72 = (f32[768]{0:T(1024)S(1)}, f32[2080]{0:T(1024)S(1)}, f32[768]{0:T(1024)S(1)}, f32[2080,768]{1,0:T(8,128)}) fusion(f32[2080,768]{1,0:T(8,128)} %get-tuple-element.242, f32[768]{0:T(1024)S(1)} %copy-done.29, f32[2080]{0:T(1024)S(1)} %copy-done.17, f32[2080]{0:T(1024)S(1)} %copy-done.15, bf16[5,416,768]{2,1,0:T(8,128)(2,1)S(1)} %copy-done.4, ...), kind=kOutput, calls=%fused_computation.135 | convolution fusion | flops 7375376384 | bytes 29132160 | tf_op jit(solution)/shard_map/nc,dc->nd/dot_general | solution.py:218
  688.7 58.4 %all-reduce.16 = (bf16[768]{0:T(1024)(128)(2,1)S(1)}, bf16[768]{0:T(1024)(128)(2,1)S(1)}, bf16[1536]{0:T(1024)(128)(2,1)S(1)}, bf16[768]{0:T(1024)(128)(2,1)S(1)...) all-reduce(f32[768]{0:T(1024)S(1)} %get-tuple-element.167, ...), channel_id=2, replica_groups=mesh['fsdp'=16,'dp'=2] {'fsdp'}, use_global_device_ids=true, to_apply=%region_16.17.clone | all-reduce | flops 9216 | bytes 55296
  747.7 4.9 all-reduce.18
  756.7 7.1 add_add_fusion
  767.2 16.9 %add_convert_fusion.2 = bf16[2080,768]{1,0:T(8,128)(2,1)} fusion(f32[2080,768]{1,0:T(8,128)} %fusion.67, bf16[2080,3072]{1,0:T(8,128)(2,1)} %get-tuple-element.234, bf16[3072,768]{1,0:T(8,128)(2,1)} %all-gather.11.cloned.1.call-done, f32[768]{0:T(1024)S(1)} %convert_element_type.205), kind=kOutput, calls=%fused_computation.105 | convolution fusion | flops 9819463680 | bytes 27085824 | tf_op jit(solution)/shard_map/dot_general | solution.py:130
  787.4 36.4 %reduce-scatter.9.cloned.1.call-done = f32[48,3072]{1,0:T(8,128)} async-done(((f32[768,3072]{1,0:T(8,128)}), f32[48,3072]{1,0:T(8,128)}) %reduce-scatter.9.cloned.1.call-update) | async-done | bytes 589840 | tf_op jit(solution)/shard_map/reduce_scatter | solution.py:170
  825.6 113.2 %reduce-scatter.11.cloned.1.call-done = f32[192,768]{1,0:T(8,128)} async-done(((f32[3072,768]{1,0:T(8,128)}), f32[192,768]{1,0:T(8,128)}) %reduce-scatter.11.cloned.1.call-update) | async-done | bytes 589840 | tf_op jit(solution)/shard_map/reduce_scatter | solution.py:172
  940.7 6.9 add_convert_fusion.1
  947.6 31.1 %all-reduce.22.cloned.1.call-done = (bf16[48,2304]{1,0:T(8,128)(2,1)}, bf16[48,768]{1,0:T(8,128)(2,1)}, bf16[48,3072]{1,0:T(8,128)(2,1)}, bf16[192,768]{1,0:T(8,128)(2,1)}) async-done(((bf16[48,2304]{1,0:T(8,128)(2,1)}, bf16[48,768]{1,0:T(8,128)(2,1)}, bf16[48,3072]{1,0:T(8,128)(2,1)}, bf16[192,768]{1,0:T(8,128)(2,1)}), (bf16[48,2304]{1,0:T(8,128)(2,1)}, bf16[48,768]{1,0:T(8,128)(2,1)}, ...) | async-done | bytes 884752 | tf_op jit(solution)/shard_map/psum | solution.py:242
  (256 shorter events, 151.5 us)
Async XLA Ops:
  7.2 8.5 copy-start.41
  7.2 79.5 %copy-start.2 = (bf16[5,416,768]{2,1,0:T(8,128)(2,1)S(1)}, bf16[5,416,768]{2,1,0:T(8,128)(2,1)}, u32[]{:S(2)}) copy-start(bf16[5,416,768]{2,1,0:T(8,128)(2,1)} %param.19) | copy-start | bytes 9584644
  7.2 11.0 %copy-start.42 = (bf16[48]{0:T(256)(128)(2,1)S(1)}, bf16[48]{0:T(256)(128)(2,1)}, u32[]{:S(2)}) copy-start(bf16[48]{0:T(256)(128)(2,1)} %param.21) | copy-start | bytes 292
  7.2 11.2 %copy-start.43 = (bf16[48]{0:T(256)(128)(2,1)S(1)}, bf16[48]{0:T(256)(128)(2,1)}, u32[]{:S(2)}) copy-start(bf16[48]{0:T(256)(128)(2,1)} %param.22) | copy-start | bytes 292
  7.2 11.5 %copy-start.44 = (bf16[48]{0:T(256)(128)(2,1)S(1)}, bf16[48]{0:T(256)(128)(2,1)}, u32[]{:S(2)}) copy-start(bf16[48]{0:T(256)(128)(2,1)} %param.26) | copy-start | bytes 292
  7.2 11.7 %copy-start.45 = (bf16[48]{0:T(256)(128)(2,1)S(1)}, bf16[48]{0:T(256)(128)(2,1)}, u32[]{:S(2)}) copy-start(bf16[48]{0:T(256)(128)(2,1)} %param.27) | copy-start | bytes 292
  7.2 11.9 %copy-start.46 = (bf16[48]{0:T(256)(128)(2,1)S(1)}, bf16[48]{0:T(256)(128)(2,1)}, u32[]{:S(2)}) copy-start(bf16[48]{0:T(256)(128)(2,1)} %param.28) | copy-start | bytes 292
  7.3 12.1 %copy-start.47 = (bf16[48]{0:T(256)(128)(2,1)S(1)}, bf16[48]{0:T(256)(128)(2,1)}, u32[]{:S(2)}) copy-start(bf16[48]{0:T(256)(128)(2,1)} %param.32) | copy-start | bytes 292
  7.3 12.4 %copy-start.48 = (bf16[192]{0:T(256)(128)(2,1)S(1)}, bf16[192]{0:T(256)(128)(2,1)}, u32[]{:S(2)}) copy-start(bf16[192]{0:T(256)(128)(2,1)} %param.30) | copy-start | bytes 1156
  7.3 12.6 %copy-start.49 = (bf16[96]{0:T(256)(128)(2,1)S(1)}, bf16[96]{0:T(256)(128)(2,1)}, u32[]{:S(2)}) copy-start(bf16[96]{0:T(256)(128)(2,1)} %param.24) | copy-start | bytes 580
  7.3 84.4 %all-gather.5.cloned.1.call-start = ((), (), s32[]{:S(2)}) async-start(), calls=%async_computation.4 | async-start | bytes 3760128 | tf_op jit(solution)/shard_map/all_gather | solution.py:85
  8.0 237.3 %all-gather.7.cloned.1.call-start = ((), (), s32[]{:S(2)}) async-start(), calls=%async_computation.5 | async-start | bytes 1253376 | tf_op jit(solution)/shard_map/all_gather | solution.py:87
  8.8 251.8 %all-gather.9.cloned.1.call-start = ((), (), s32[]{:S(2)}) async-start(), calls=%async_computation.6 | async-start | bytes 5013504 | tf_op jit(solution)/shard_map/all_gather | solution.py:113
  9.5 322.6 %all-gather.11.cloned.1.call-start = ((), (), s32[]{:S(2)}) async-start(), calls=%async_computation.7 | async-start | bytes 5013504 | tf_op jit(solution)/shard_map/all_gather | solution.py:115
  10.1 774.1 %reduce-scatter.7.cloned.1.call-start = ((), (), s32[]{:S(2)}) async-start(), calls=%async_computation.9 | async-start | bytes 2506752 | tf_op jit(solution)/shard_map/reduce_scatter | solution.py:236
  15.6 76.1 %copy-start.14 = (f32[2080]{0:T(1024)}, f32[2080]{0:T(1024)S(1)}, u32[]{:S(2)}) copy-start(f32[2080]{0:T(1024)S(1)} %div.47) | copy-start | bytes 24964
  84.2 7.5 copy-start.28
  84.2 7.5 copy-start.24
  84.3 7.4 copy-start.16
  136.1 10.8 %copy-start.10 = (bf16[2080,768]{1,0:T(8,128)(2,1)S(1)}, bf16[2080,768]{1,0:T(8,128)(2,1)}, u32[]{:S(2)}) copy-start(bf16[2080,768]{1,0:T(8,128)(2,1)} %slice.33) | copy-start | bytes 9584644
  235.7 9.7 copy-start.3
  235.7 9.7 copy-start.37
  253.1 7.5 copy-start.30
  253.1 7.5 copy-start.33
  253.1 7.6 copy-start.35
  256.3 126.3 %copy-start.20 = (f32[2080]{0:T(1024)}, f32[2080]{0:T(1024)S(1)}, u32[]{:S(2)}) copy-start(f32[2080]{0:T(1024)S(1)} %broadcast_multiply_fusion.1) | copy-start | bytes 24964
  259.9 0.6 copy-start.22
  260.6 122.0 %copy-start.26 = (f32[2080]{0:T(1024)}, f32[2080]{0:T(1024)S(1)}, u32[]{:S(2)}) copy-start(f32[2080]{0:T(1024)S(1)} %fusion.69) | copy-start | bytes 24964
  260.6 71.5 %copy-start.5 = (bf16[5,416,768]{2,1,0:T(8,128)(2,1)S(1)}, bf16[5,416,768]{2,1,0:T(8,128)(2,1)}, u32[]{:S(2)}) copy-start(bf16[5,416,768]{2,1,0:T(8,128)(2,1)} %param.33) | copy-start | bytes 9584644
  360.5 22.1 %copy-start.23 = (f32[2080]{0:T(1024)S(1)}, f32[2080]{0:T(1024)}, u32[]{:S(2)}) copy-start(f32[2080]{0:T(1024)} %copy-done.22) | copy-start | bytes 24964
  360.5 22.1 %copy-start.1 = (f32[2080,768]{1,0:T(8,128)S(1)}, f32[2080,768]{1,0:T(8,128)}, u32[]{:S(2)}) copy-start(f32[2080,768]{1,0:T(8,128)} %fusion.67) | copy-start | bytes 19169284
  387.5 5.6 copy-start
  387.5 5.5 copy-start.18
  387.5 5.5 copy-start.11
  424.2 361.5 %reduce-scatter.5.cloned.1.call-start = ((), (), s32[]{:S(2)}) async-start(), calls=%async_computation.8 | async-start | bytes 7520256 | tf_op jit(solution)/shard_map/reduce_scatter | solution.py:234
  603.3 1.9 copy-start.8
  603.3 3.0 copy-start.9
  605.2 5.3 copy-start.12
  606.7 3.8 copy-start.13
  621.5 0.7 copy-start.21
  621.5 0.7 copy-start.27
  621.5 0.7 copy-start.31
  621.5 0.7 copy-start.36
  621.6 202.2 %reduce-scatter.9.cloned.1.call-start = ((), (), s32[]{:S(2)}) async-start(), calls=%async_computation.10 | async-start | bytes 10027008 | tf_op jit(solution)/shard_map/reduce_scatter | solution.py:170
  641.7 1.9 copy-start.6
  641.7 297.1 %reduce-scatter.11.cloned.1.call-start = ((), (), s32[]{:S(2)}) async-start(), calls=%async_computation.11 | async-start | bytes 10027008 | tf_op jit(solution)/shard_map/reduce_scatter | solution.py:172
  659.3 2.4 copy-start.40
  659.3 9.5 copy-start.4
  659.3 9.5 copy-start.15
  659.3 9.5 copy-start.17
  659.3 9.5 copy-start.29
  659.4 319.4 %all-reduce.22.cloned.1.call-start = ((), (), s32[]{:S(2)}) async-start(), calls=%async_computation.12 | async-start | bytes 1769472 | tf_op jit(solution)/shard_map/psum | solution.py:242
  668.9 19.6 %copy-start.32 = (f32[768]{0:T(1024)S(1)}, f32[768]{0:T(1024)}, u32[]{:S(2)}) copy-start(f32[768]{0:T(1024)} %get-tuple-element.230) | copy-start | bytes 9220
  668.9 19.6 %copy-start.34 = (f32[3072]{0:T(1024)S(1)}, f32[3072]{0:T(1024)}, u32[]{:S(2)}) copy-start(f32[3072]{0:T(1024)} %get-tuple-element.251) | copy-start | bytes 36868
  668.9 19.6 %copy-start.38 = (f32[768]{0:T(1024)S(1)}, f32[768]{0:T(1024)}, u32[]{:S(2)}) copy-start(f32[768]{0:T(1024)} %get-tuple-element.162) | copy-start | bytes 9220
  668.9 19.6 %copy-start.39 = (f32[768]{0:T(1024)S(1)}, f32[768]{0:T(1024)}, u32[]{:S(2)}) copy-start(f32[768]{0:T(1024)} %get-tuple-element.164) | copy-start | bytes 9220
  668.9 87.8 %copy-start.25 = (f32[2080]{0:T(1024)S(1)}, f32[2080]{0:T(1024)}, u32[]{:S(2)}) copy-start(f32[2080]{0:T(1024)} %copy-done.24) | copy-start | bytes 24964
  767.2 173.5 %copy-start.7 = (bf16[5,416,768]{2,1,0:T(8,128)(2,1)S(1)}, bf16[5,416,768]{2,1,0:T(8,128)(2,1)}, u32[]{:S(2)}) copy-start(bf16[5,416,768]{2,1,0:T(8,128)(2,1)} %param.33) | copy-start | bytes 9584644
  767.2 173.5 %copy-start.19 = (f32[2080]{0:T(1024)S(1)}, f32[2080]{0:T(1024)}, u32[]{:S(2)}) copy-start(f32[2080]{0:T(1024)} %copy-done.18) | copy-start | bytes 24964
Sparse Core Ops, SparseCore 0:
  10.4 50.3 all-gather.4
  63.1 36.6 all-gather.6
  102.1 51.9 all-gather.8
  156.3 51.6 all-gather.10
  424.3 60.4 reduce-scatter.6
  621.7 87.2 reduce-scatter.4
  713.1 110.7 reduce-scatter.8
  827.9 110.8 reduce-scatter.10
  942.5 36.2 all-reduce.21
where the time goes:
time: 1000 us; the launch traced here: 992 us
  matrix products  370 us (37%)
  local copies, waits for them, and re-layouts  185 us (18%)
  waiting for transfers between devices  183 us (18%)
  blocking collectives  127 us (13%)
  other arithmetic  107 us (11%)
  between operations  18.9 us (2%)
    unnamed x2, blocking collectives  122 us
    reduce_scatter x1, waiting for transfers between devices, per_device(): lax.psum_scatter(mlp_local[4], 'fsdp', scatter_dimension=0, tiled=True)  113 us
    dot_general x1, matrix products, per_device(): jnp.dot(normed_two_low, up_full, preferred_element_type=jnp.float32)  71.5 us
    while x4, local copies, waits for them, and re-layouts, per_device(): lax.map(row_forward, (queries, keys_all, values_all, segment_ids))  39.8 us
    reduce_scatter x1, waiting for transfers between devices, per_device(): lax.psum_scatter(mlp_local[2], 'fsdp', scatter_dimension=0, tiled=True)  36.4 us
    while x4, local copies, waits for them, and re-layouts, per_device(): lax.map(row_backward, (queries, keys_all, values_all, segment_ids, grad_m...  33.9 us
    psum x1, waiting for transfers between devices, per_device(): lax.psum(attn_owned[2].astype(jnp.bfloat16), 'dp').astype(jnp.float32)  31.1 us
    dot_general x10, matrix products, masked_scores(): jnp.einsum('qhe,khe->hqk', queries, keys_row, preferred_element_type=jnp....  31.1 us
  transfers between devices with their start and end apart: 9, of which 3 were waited for; matrix products, arithmetic and copies ran while one was open for 56% of the time, Pallas kernels for 0%

commit v1 on v0

v1 whole, which is shorter than its diff:
```python
import jax
import jax.numpy as jnp
from jax import lax
from jax.experimental import pallas as pl
from jax.experimental.pallas import tpu as pltpu
from jax.sharding import PartitionSpec as P

HEAD_DIM = 64
F32 = jnp.float32
BF16 = jnp.bfloat16
VMEM_LIMIT = 60 * 1024 * 1024
NT = (((1,), (1,)), ((), ()))
TN = (((0,), (0,)), ((), ()))


def dot(left, right):
    return jnp.dot(left, right, preferred_element_type=F32)


def dot_nt(left, right):
    return lax.dot_general(left, right, NT, preferred_element_type=F32)


def dot_tn(left, right):
    return lax.dot_general(left, right, TN, preferred_element_type=F32)


def norm_parts(values):
    center = values - jnp.mean(values, axis=-1, keepdims=True)
    inv = lax.rsqrt(jnp.mean(center * center, axis=-1, keepdims=True) + 1e-06)
    return center * inv, inv


def norm_grad(xhat, inv, grad, gain):
    scaled = grad * gain
    first = jnp.mean(scaled, axis=-1, keepdims=True)
    second = jnp.mean(scaled * xhat, axis=-1, keepdims=True)
    return inv * (scaled - first - xhat * second)


def half_masks(width):
    lane = lax.broadcasted_iota(jnp.int32, (1, width), 1)
    return (lane % (2 * HEAD_DIM)) < HEAD_DIM


def attn_fwd_kernel(
    x_ref, segc_ref, segr_ref, w_ref, gain_ref, shift_ref, bias_ref,
    h1_ref, qkv_ref, p_ref, mixed_ref, kz_ref, vt_ref, mt_ref, mask_ref,
):
    width = x_ref.shape[1]
    heads = width // HEAD_DIM
    xhat, _ = norm_parts(x_ref[...].astype(F32))
    h1 = (xhat * gain_ref[...] + shift_ref[...]).astype(BF16)
    h1_ref[...] = h1
    low = half_masks(width)
    q = (dot(h1, w_ref[:, :width]) + bias_ref[:, :width]).astype(BF16)
    qkv_ref[:, :width] = q * jnp.asarray(0.125, BF16)
    k = dot(h1, w_ref[:, width : 2 * width]).astype(BF16)
    qkv_ref[:, width : 2 * width] = k
    zero = jnp.zeros_like(k)
    kz_ref[0] = jnp.where(low, k, zero)
    kz_ref[1] = jnp.where(low, zero, k)
    v = (dot(h1, w_ref[:, 2 * width : 3 * width]) + bias_ref[:, width:]).astype(BF16)
    qkv_ref[:, 2 * width :] = v
    vt_ref[...] = v.T
    mask_ref[...] = jnp.where(segc_ref[...] == segr_ref[...], 0.0, -1e30)
    for head in range(heads):
        pair = slice(head // 2 * 128, head // 2 * 128 + 128)
        rows = slice(head * HEAD_DIM, (head + 1) * HEAD_DIM)
        scores = dot_nt(kz_ref[head % 2, :, pair], qkv_ref[:, pair]) + mask_ref[...]
        expo = jnp.exp(scores - jnp.max(scores, axis=0, keepdims=True))
        total = jnp.sum(expo, axis=0, keepdims=True)
        probs = (expo * (1.0 / total)).astype(BF16)
        p_ref[head] = probs
        mt_ref[rows, :] = dot(vt_ref[rows, :], probs)
    mixed_ref[...] = mt_ref[...].T.astype(BF16)


def attn_bwd_kernel(
    qkv_ref, p_ref, mixed_ref, do_ref, dproj_ref, dbias_ref, vz_ref, kt_ref, dqt_ref, d_ref,
):
    width = mixed_ref.shape[1]
    heads = width // HEAD_DIM
    low = half_masks(width)
    v = qkv_ref[:, 2 * width :]
    zero = jnp.zeros_like(v)
    vz_ref[0] = jnp.where(low, v, zero)
    vz_ref[1] = jnp.where(low, zero, v)
    kt_ref[...] = qkv_ref[:, width : 2 * width].T
    prod = (do_ref[...].astype(F32) * mixed_ref[...].astype(F32)).T
    d_ref[...] = jnp.sum(prod.reshape(heads, HEAD_DIM, prod.shape[1]), axis=1)
    low_pair = half_masks(2 * HEAD_DIM)
    for pair_index in range(heads // 2):
        pair = slice(pair_index * 128, pair_index * 128 + 128)
        dvs, dks = [], []
        for half in range(2):
            head = 2 * pair_index + half
            rows = slice(head * HEAD_DIM, (head + 1) * HEAD_DIM)
            dprobs = dot_nt(vz_ref[half, :, pair], do_ref[:, pair])
            probs = p_ref[head]
            dvs.append(dot(probs, do_ref[:, pair]))
            dscores = (probs.astype(F32) * (dprobs - d_ref[head : head + 1, :])).astype(BF16)
            dks.append(dot(dscores, qkv_ref[:, pair]))
            dqt_ref[rows, :] = dot(kt_ref[rows, :], dscores)
        start = width + pair_index * 128
        dproj_ref[:, start : start + 128] = jnp.where(low_pair, dks[0], dks[1]).astype(BF16)
        start = 2 * width + pair_index * 128
        dproj_ref[:, start : start + 128] = jnp.where(low_pair, dvs[0], dvs[1]).astype(BF16)
    dq = (dqt_ref[...] * 0.125).T.astype(BF16)
    dproj_ref[:, :width] = dq

    @pl.when(pl.program_id(0) == 0)
    def _():
        dbias_ref[...] = jnp.zeros_like(dbias_ref)

    dbias_ref[:, :width] += jnp.sum(dq.astype(F32), axis=0, keepdims=True)
    dbias_ref[:, width:] += jnp.sum(dproj_ref[:, 2 * width :].astype(F32), axis=0, keepdims=True)


def mlp_kernel(
    x_ref, att_ref, dy_ref, wo_ref, wu_ref, wd_ref, bo_ref, gain_ref, shift_ref, bu_ref, bd_ref,
    out_ref, h2_ref, act_ref, dpre_ref, dz_ref, datt_ref, dsmall_ref, dbu_ref,
):
    width = x_ref.shape[1]
    hidden = wu_ref.shape[1]
    chunk = 512 if hidden % 512 == 0 else 128
    middle = x_ref[...].astype(F32) + dot(att_ref[...], wo_ref[...]) + bo_ref[...]
    xhat, inv = norm_parts(middle)
    h2 = (xhat * gain_ref[...] + shift_ref[...]).astype(BF16)
    h2_ref[...] = h2
    dy = dy_ref[...]
    out = middle + bd_ref[...]
    dh2 = None

    @pl.when(pl.program_id(0) == 0)
    def _():
        dsmall_ref[...] = jnp.zeros_like(dsmall_ref)
        dbu_ref[...] = jnp.zeros_like(dbu_ref)

    for start in range(0, hidden, chunk):
        cols = slice(start, start + chunk)
        pre = dot(h2, wu_ref[:, cols]) + bu_ref[:, cols]
        dact = dot_nt(dy, wd_ref[cols, :])
        cdf = 0.5 * (1.0 + lax.erf(pre * 0.7071067811865476))
        pdf = jnp.exp(-0.5 * pre * pre) * 0.3989422804014327
        act = (pre * cdf).astype(BF16)
        dpre = dact * (cdf + pre * pdf)
        act_ref[:, cols] = act
        dbu_ref[:, cols] += jnp.sum(dpre, axis=0, keepdims=True)
        dpre = dpre.astype(BF16)
        dpre_ref[:, cols] = dpre
        out += dot(act, wd_ref[cols, :])
        part = dot_nt(dpre, wu_ref[:, cols])
        dh2 = part if dh2 is None else dh2 + part
    out_ref[...] = out.astype(BF16)
    wide_dy = dy.astype(F32)
    dmiddle = wide_dy + norm_grad(xhat, inv, dh2, gain_ref[...])
    dz = dmiddle.astype(BF16)
    dz_ref[...] = dz
    datt_ref[...] = dot_nt(dz, wo_ref[...]).astype(BF16)
    dsmall_ref[0:1, :] += jnp.sum(dz.astype(F32), axis=0, keepdims=True)
    dsmall_ref[1:2, :] += jnp.sum(dh2 * xhat, axis=0, keepdims=True)
    dsmall_ref[2:3, :] += jnp.sum(dh2, axis=0, keepdims=True)
    dsmall_ref[3:4, :] += jnp.sum(wide_dy, axis=0, keepdims=True)


def input_grad_kernel(x_ref, dproj_ref, dz_ref, w_ref, gain_ref, dx_ref, dsmall_ref):
    width = x_ref.shape[1]
    dh1 = dot_nt(dproj_ref[...], w_ref[:, : 3 * width])
    xhat, inv = norm_parts(x_ref[...].astype(F32))
    dx = dz_ref[...].astype(F32) + norm_grad(xhat, inv, dh1, gain_ref[...])
    dx_ref[...] = dx.astype(BF16)

    @pl.when(pl.program_id(0) == 0)
    def _():
        dsmall_ref[...] = jnp.zeros_like(dsmall_ref)

    dsmall_ref[0:1, :] += jnp.sum(dh1 * xhat, axis=0, keepdims=True)
    dsmall_ref[1:2, :] += jnp.sum(dh1, axis=0, keepdims=True)


def row_spec(*shape):
    return pl.BlockSpec((None,) + shape, lambda i: (i,) + (0,) * len(shape))


def whole(*shape):
    return pl.BlockSpec(shape, lambda i: (0,) * len(shape), pipeline_mode=pl.Buffered(1))


def acc_spec(*shape):
    return pl.BlockSpec(shape, lambda i: (0,) * len(shape))


def sds(shape, dtype):
    return jax.ShapeDtypeStruct(shape, dtype)


def run(kernel, grid, in_specs, outs, out_specs, scratch, args, flops, name):
    total = sum(a.size * a.dtype.itemsize for a in args)
    total += sum(o.size * jnp.dtype(o.dtype).itemsize for o in outs)
    return pl.pallas_call(
        kernel,
        grid=grid,
        in_specs=in_specs,
        out_specs=out_specs,
        out_shape=outs,
        scratch_shapes=scratch,
        compiler_params=pltpu.CompilerParams(
            dimension_semantics=("arbitrary",), vmem_limit_bytes=VMEM_LIMIT
        ),
        cost_estimate=pl.CostEstimate(flops=flops, bytes_accessed=total, transcendentals=0),
        name=name,
    )(*args)


def attn_fwd(x, segs, w, gain, shift, bias):
    rows, slots, width = x.shape
    heads = width // HEAD_DIM
    outs = (
        sds((rows, slots, width), BF16),
        sds((rows, slots, 3 * width), BF16),
        sds((rows, heads, slots, slots), BF16),
        sds((rows, slots, width), BF16),
    )
    return run(
        attn_fwd_kernel,
        (rows,),
        [
            row_spec(slots, width),
            row_spec(slots, 1),
            row_spec(1, slots),
            whole(width, 3 * width),
            whole(1, width),
            whole(1, width),
            whole(1, 2 * width),
        ],
        outs,
        [
            row_spec(slots, width),
            row_spec(slots, 3 * width),
            row_spec(heads, slots, slots),
            row_spec(slots, width),
        ],
        [
            pltpu.VMEM((2, slots, width), BF16),
            pltpu.VMEM((width, slots), BF16),
            pltpu.VMEM((width, slots), F32),
            pltpu.VMEM((slots, slots), F32),
        ],
        (x, segs[:, :, None], segs[:, None, :], w, gain, shift, bias),
        rows * (6 * slots * width * width + 4 * slots * slots * width * 4),
        "attn_fwd",
    )


def attn_bwd(qkv, probs, mixed, dmixed):
    rows, slots, width = mixed.shape
    heads = width // HEAD_DIM
    return run(
        attn_bwd_kernel,
        (rows,),
        [
            row_spec(slots, 3 * width),
            row_spec(heads, slots, slots),
            row_spec(slots, width),
            row_spec(slots, width),
        ],
        (sds((rows, slots, 3 * width), BF16), sds((1, 2 * width), F32)),
        [row_spec(slots, 3 * width), acc_spec(1, 2 * width)],
        [
            pltpu.VMEM((2, slots, width), BF16),
            pltpu.VMEM((width, slots), BF16),
            pltpu.VMEM((width, slots), F32),
            pltpu.VMEM((heads, slots), F32),
        ],
        (qkv, probs, mixed, dmixed),
        rows * 8 * slots * slots * width * 4,
        "attn_bwd",
    )


def mlp(x, mixed, dy, wo, wu, wd, bo, gain, shift, bu, bd):
    rows, slots, width = x.shape
    hidden = wu.shape[1]
    act = row_spec(slots, width)
    wide = row_spec(slots, hidden)
    return run(
        mlp_kernel,
        (rows,),
        [
            act, act, act,
            whole(width, width), whole(width, hidden), whole(hidden, width),
            whole(1, width), whole(1, width), whole(1, width), whole(1, hidden), whole(1, width),
        ],
        (
            sds(x.shape, BF16), sds(x.shape, BF16), sds((rows, slots, hidden), BF16),
            sds((rows, slots, hidden), BF16), sds(x.shape, BF16), sds(x.shape, BF16),
            sds((8, width), F32), sds((1, hidden), F32),
        ),
        [act, act, wide, wide, act, act, acc_spec(8, width), acc_spec(1, hidden)],
        [],
        (x, mixed, dy, wo, wu, wd, bo, gain, shift, bu, bd),
        rows * slots * width * (8 * hidden + 4 * width),
        "mlp",
    )


def input_grad(x, dproj, dz, w, gain):
    rows, slots, width = x.shape
    act = row_spec(slots, width)
    return run(
        input_grad_kernel,
        (rows,),
        [act, row_spec(slots, 3 * width), act, whole(width, 3 * width), whole(1, width)],
        (sds(x.shape, BF16), sds((8, width), F32)),
        [act, acc_spec(8, width)],
        [],
        (x, dproj, dz, w, gain),
        rows * slots * width * width * 6,
        "input_grad",
    )


def gather(shard):
    return lax.all_gather(shard, "fsdp", axis=0, tiled=True)


def scatter(full):
    owned = lax.psum_scatter(full, "fsdp", scatter_dimension=0, tiled=True)
    return lax.psum(owned, "dp").astype(F32)


def weight_grad(left, right):
    flat_left = left.reshape(-1, left.shape[-1])
    flat_right = right.reshape(-1, right.shape[-1])
    return dot_tn(flat_left, flat_right).astype(BF16)


def per_device(
    block_input, segment_ids, ln1_gain, ln1_bias, qkv_weight, qv_bias, out_weight, out_bias,
    ln2_gain, ln2_bias, up_weight, up_bias, down_weight, down_bias, out_cotangent,
):
    rows, slots, width = block_input.shape
    shard = ln1_gain.shape[0]
    parts = width // shard
    small = jnp.concatenate(
        [
            ln1_gain, ln1_bias, qv_bias, out_bias, ln2_gain, ln2_bias, up_bias, down_bias,
        ]
    )[None]
    sizes = [shard, shard, 2 * shard, shard, shard, shard, 4 * shard, shard]
    small_full = gather(small).astype(F32)
    vectors, start = [], 0
    for size in sizes:
        vectors.append(small_full[:, start : start + size].reshape(1, size * parts))
        start += size
    gain1, shift1, bias_qv, bias_out, gain2, shift2, bias_up, bias_down = vectors
    w_qkv = gather(qkv_weight)
    w_out = gather(out_weight)
    w_up = gather(up_weight)
    w_down = gather(down_weight)

    h1, qkv, probs, mixed = attn_fwd(block_input, segment_ids, w_qkv, gain1, shift1, bias_qv)
    out, h2, act, dpre, dz, dmixed, dsmall2, dbias_up = mlp(
        block_input, mixed, out_cotangent, w_out, w_up, w_down,
        bias_out, gain2, shift2, bias_up, bias_down,
    )
    down_grad = scatter(weight_grad(act, out_cotangent))
    up_grad = scatter(weight_grad(h2, dpre))
    out_grad = scatter(weight_grad(mixed, dz))
    dproj, dbias_qv = attn_bwd(qkv, probs, mixed, dmixed)
    qkv_grad = scatter(weight_grad(h1, dproj))
    dx, dsmall1 = input_grad(block_input, dproj, dz, w_qkv, gain1)
    grads = [
        dsmall1[0:1], dsmall1[1:2], dbias_qv, dsmall2[0:1],
        dsmall2[1:2], dsmall2[2:3], dbias_up, dsmall2[3:4],
    ]
    packed = jnp.concatenate([g.reshape(parts, -1) for g in grads], axis=1)
    owned = lax.psum_scatter(packed, "fsdp", scatter_dimension=0, tiled=True)
    owned = lax.psum(owned, "dp")[0]
    pieces, start = [], 0
    for size in sizes:
        pieces.append(owned[start : start + size])
        start += size
    return (
        out, dx, pieces[0], pieces[1], qkv_grad, pieces[2], out_grad, pieces[3],
        pieces[4], pieces[5], up_grad, pieces[6], down_grad, pieces[7],
    )


def solution(mesh):
    both = ("fsdp", "dp")
    vec, mat, act = P("fsdp"), P("fsdp", None), P(both, None, None)
    return jax.shard_map(
        per_device,
        mesh=mesh,
        in_specs=(
            act, P(both, None), vec, vec, mat, vec, mat, vec, vec, vec, mat, vec, mat, vec, act,
        ),
        out_specs=(act, act, vec, vec, mat, vec, mat, vec, vec, vec, mat, vec, mat, vec),
        check_vma=False,
    )
```

time: 1000 us -> 669 us (0.67)
  matrix products: 370 us -> 51.3 us
  local copies, waits for them, and re-layouts: 185 us -> 24.4 us
  Pallas kernels: 0 us -> 157 us
  other arithmetic: 107 us -> 7.61 us
  waiting for transfers between devices: 183 us -> 279 us
    dot_general x47 -> x4, matrix products: 370 us -> 51.3 us  [dot_tn(): return lax.dot_general(left, right, TN, preferred_element_type=F32)]
    pallas_call x0 -> x4, Pallas kernels: none -> 157 us  [run(): pl.pallas_call(kernel, grid=grid, in_specs=in_specs, out_specs=out_specs,...]
    all_gather x4, waiting for transfers between devices: 0.06 us -> 74 us  [gather(): return lax.all_gather(shard, 'fsdp', axis=0, tiled=True)]
    while x8 -> x0, local copies, waits for them, and re-layouts: 73.8 us -> none  [the longest x4 39.8 us: per_device(): lax.map(row_forward, (queries, keys_all, values_all, segment_ids))]
    reshape x8 -> x16, local copies, waits for them, and re-layouts: 74.5 us -> 5.94 us  [the longest x8 5.36 us: per_device(): vectors.append(small_full[:, start:start + size].reshape(1, size * parts))]
    reduce_scatter x4, waiting for transfers between devices: 150 us -> 202 us  [scatter(): owned = lax.psum_scatter(full, 'fsdp', scatter_dimension=0, tiled=True)]
    reduce_sum x14 -> x0, other arithmetic: 43.8 us -> none  [the longest x4 13.8 us: layer_norm(): center = values - jnp.mean(values, axis=-1, keepdims=True)]
    convert_element_type x30 -> x4, other arithmetic: 45.7 us -> 6.91 us  [scatter(): return lax.psum(owned, 'dp').astype(F32)]
  transfers between devices with their start and end apart: 9 -> 9, of which waited for: 3 -> 5; matrix products, arithmetic and copies ran while one was open for 56% -> 10% of each run, Pallas kernels for 0% -> 14%
where the time goes in v1:
time: 669 us; the launch traced here: 662 us
  waiting for transfers between devices  279 us (42%)
  Pallas kernels  157 us (23%)
  blocking collectives  127 us (19%)
  matrix products  51.3 us (8%)
  local copies, waits for them, and re-layouts  24.4 us (4%)
  between operations  14.8 us (2%)
  other arithmetic  7.61 us (1%)
    reduce_scatter x4, waiting for transfers between devices, scatter(): owned = lax.psum_scatter(full, 'fsdp', scatter_dimension=0, tiled=True)  202 us
    pallas_call x4, Pallas kernels, run(): pl.pallas_call(kernel, grid=grid, in_specs=in_specs, out_specs=out_specs,...  157 us
    unnamed x2, blocking collectives  122 us
    all_gather x4, waiting for transfers between devices, gather(): return lax.all_gather(shard, 'fsdp', axis=0, tiled=True)  74 us
    dot_general x4, matrix products, dot_tn(): return lax.dot_general(left, right, TN, preferred_element_type=F32)  51.3 us
  transfers between devices with their start and end apart: 9, of which 5 were waited for; matrix products, arithmetic and copies ran while one was open for 10% of the time, Pallas kernels for 14%

profile of v1, /device:TPU:0, one launch (start us, length us, event | category | flops | bytes accessed | tf_op | source)
XLA Modules:
  0.0 661.7 jit_solution(9073085699529822743)
XLA Ops:
  7.2 0.7 all-gather.6.cloned.1.call-update
  8.0 0.7 all-gather.8.cloned.1.call-update
  8.7 0.7 all-gather.10.cloned.1.call-update
  9.4 0.5 all-gather.12.cloned.1.call-update
  10.0 0.0 reduce-scatter.7.cloned.1.call-start
  10.0 1.3 fusion.1
  12.0 5.4 concatenate.6
  17.4 0.2 dynamic-update-slice
  17.7 63.8 %all-reduce = bf16[9216]{0:T(1024)(128)(2,1)S(1)} all-reduce(bf16[9216]{0:T(1024)(128)(2,1)S(1)} %dynamic-update-slice), channel_id=2, replica_groups=mesh['fsdp'=16,'dp'=2] {'fsdp'}, use_global_device_ids=true, to_apply=%add | all-reduce | flops 9216 | bytes 36864
  81.5 0.1 reshape.109
  81.5 0.1 slice.122
  81.6 0.1 slice.126
  81.7 0.1 fusion
  81.8 0.7 reshape.92.gain_ref
  82.4 0.7 reshape.93.shift_ref
  83.1 0.7 reshape.94.bias_ref
  83.8 1.3 broadcast_in_dim.10.segr_ref
  85.1 2.1 copy.30.segc_ref
  87.2 0.7 reshape.95.bo_ref
  87.8 0.7 reshape.96.gain_ref
  88.5 0.7 reshape.97.shift_ref
  89.2 0.7 reshape.99.bd_ref
  89.8 0.7 reshape.98.bu_ref
  90.5 43.3 %attn_fwd.1 = (bf16[5,416,768]{2,1,0:T(8,128)(2,1)}, bf16[5,416,2304]{2,1,0:T(8,128)(2,1)}, bf16[5,12,416,416]{3,2,1,0:T(8,128)(2,1)}, bf16[5,416,768]{2,1,0:T(8,128)(2,1)}) custom-call(bf16[5,416,768]{2,1,0:T(8,128)(2,1)} %x_ref.5, s32[5,416,1]{2,1,0:T(8,128)} %copy.30.segc_ref, s32[5,1,416]{2,1,0:T(1,128)} %broadcast_in_dim.10.segr_ref, ...), custom_call_target="tpu_custom_call" | custom-call | flops 17993564160 | bytes 43503872 | tf_op jit(solution)/shard_map/attn_fwd/pallas_call | solution.py:201
  133.8 20.1 %all-gather.10.cloned.1.call-done.wu_ref = bf16[768,3072]{1,0:T(8,128)(2,1)} async-done(((bf16[48,3072]{1,0:T(8,128)(2,1)}), bf16[768,3072]{1,0:T(8,128)(2,1)}) %all-gather.10.cloned.1.call-update) | async-done | bytes 4718608 | tf_op jit(solution)/shard_map/all_gather | solution.py:325
  153.9 53.8 %all-gather.12.cloned.1.call-done.wd_ref = bf16[3072,768]{1,0:T(8,128)(2,1)} async-done(((bf16[192,768]{1,0:T(8,128)(2,1)}), bf16[3072,768]{1,0:T(8,128)(2,1)}) %all-gather.12.cloned.1.call-update) | async-done | bytes 4718608 | tf_op jit(solution)/shard_map/all_gather | solution.py:325
  207.8 64.6 %mlp.1 = (bf16[5,416,768]{2,1,0:T(8,128)(2,1)}, bf16[5,416,768]{2,1,0:T(8,128)(2,1)}, bf16[5,416,3072]{2,1,0:T(8,128)(2,1)}, bf16[5,416,3072]{2,1,0:T(8,128)(2,1...) custom-call(bf16[5,416,768]{2,1,0:T(8,128)(2,1)} %x_ref.5, ...), custom_call_target="tpu_custom_call" | custom-call | flops 44166021120 | bytes 58601472 | tf_op jit(solution)/shard_map/mlp/pallas_call | solution.py:201
  272.4 5.9 bitcast_convert_fusion.3
  278.3 0.0 reduce-scatter.5.cloned.1.call-start
  278.4 32.8 %attn_bwd.1 = (bf16[5,416,2304]{2,1,0:T(8,128)(2,1)}, f32[1,1536]{1,0:T(1,128)}) custom-call(bf16[5,416,2304]{2,1,0:T(8,128)(2,1)} %get-tuple-element.32.qkv_ref, bf16[5,12,416,416]{3,2,1,0:T(8,128)(2,1)} %get-tuple-element.33.p_ref, bf16[5,416,768]{2,1,0:T(8,128)(2,1)} %get-tuple-element.30.att_ref.mixed_ref, bf16[5,416,768]{2,1,0:T(8,128)(2,1)} %get-tuple-element.34.do_ref), custom_call_target="tpu_custom_call" | custom-call | flops 21265121280 | bytes 46331904 | tf_op jit(solution)/shard_map/attn_bwd/pallas_call | solution.py:201
  311.2 13.2 %bitcast_convert_fusion.2 = bf16[768,2304]{1,0:T(8,128)(2,1)} fusion(bf16[5,416,768]{2,1,0:T(8,128)(2,1)S(1)} %copy-done.6, bf16[5,416,2304]{2,1,0:T(8,128)(2,1)} %get-tuple-element.35.dproj_ref), kind=kOutput, calls=%fused_computation.2 | convolution fusion | flops 7362772992 | bytes 16318464 | tf_op jit(solution)/shard_map/dot_general | solution.py:25
  324.5 0.0 reduce-scatter.9.cloned.1.call-start
  324.5 1.8 copy-done.5
  326.4 16.1 %bitcast_convert_fusion.1 = bf16[768,3072]{1,0:T(8,128)(2,1)} fusion(bf16[5,416,768]{2,1,0:T(8,128)(2,1)S(1)} %copy-done.5, bf16[5,416,3072]{2,1,0:T(8,128)(2,1)} %get-tuple-element.44), kind=kOutput, calls=%fused_computation.1 | convolution fusion | flops 9817030656 | bytes 20692992 | tf_op jit(solution)/shard_map/dot_general | solution.py:25
  342.5 0.0 reduce-scatter.11.cloned.1.call-start
  342.5 2.0 copy-done.3
  344.5 16.1 %bitcast_convert_fusion = bf16[3072,768]{1,0:T(8,128)(2,1)} fusion(bf16[5,416,3072]{2,1,0:T(8,128)(2,1)} %get-tuple-element.45, bf16[5,416,768]{2,1,0:T(8,128)(2,1)S(1)} %copy-done.3), kind=kOutput, calls=%fused_computation | convolution fusion | flops 9817030656 | bytes 20692992 | tf_op jit(solution)/shard_map/dot_general | solution.py:25
  360.6 0.0 all-reduce.5.cloned.1.call-start
  360.7 45.5 %reduce-scatter.5.cloned.1.call-done = bf16[48,2304]{1,0:T(8,128)(2,1)} async-done(((bf16[768,2304]{1,0:T(8,128)(2,1)}), bf16[48,2304]{1,0:T(8,128)(2,1)}) %reduce-scatter.5.cloned.1.call-update) | async-done | bytes 221200 | tf_op jit(solution)/shard_map/reduce_scatter | solution.py:329
  406.1 78.2 %reduce-scatter.9.cloned.1.call-done = bf16[48,3072]{1,0:T(8,128)(2,1)} async-done(((bf16[768,3072]{1,0:T(8,128)(2,1)}), bf16[48,3072]{1,0:T(8,128)(2,1)}) %reduce-scatter.9.cloned.1.call-update) | async-done | bytes 294928 | tf_op jit(solution)/shard_map/reduce_scatter | solution.py:329
  484.4 78.7 %reduce-scatter.11.cloned.1.call-done = bf16[192,768]{1,0:T(8,128)(2,1)} async-done(((bf16[3072,768]{1,0:T(8,128)(2,1)}), bf16[192,768]{1,0:T(8,128)(2,1)}) %reduce-scatter.11.cloned.1.call-update) | async-done | bytes 294928 | tf_op jit(solution)/shard_map/reduce_scatter | solution.py:329
  563.1 16.4 %input_grad.1 = (bf16[5,416,768]{2,1,0:T(8,128)(2,1)}, f32[8,768]{1,0:T(8,128)}) custom-call(bf16[5,416,768]{2,1,0:T(8,128)(2,1)} %x_ref.5, bf16[5,416,2304]{2,1,0:T(8,128)(2,1)} %get-tuple-element.35.dproj_ref, bf16[5,416,768]{2,1,0:T(8,128)(2,1)} %get-tuple-element.36.dz_ref, bf16[768,2304]{1,0:T(8,128)(2,1)} %all-gather.6.cloned.1.call-done.w_ref, ...), custom_call_target="tpu_custom_call" | custom-call | flops 7361003520 | bytes 22735872 | tf_op jit(solution)/shard_map/input_grad/pallas_call | solution.py:201
  579.5 0.8 slice_reduce_fusion.4
  580.4 0.1 reshape.100
  580.5 0.1 reshape.101
  580.6 0.1 reshape.102
  580.7 0.1 reshape.103
  580.7 0.1 reshape.104
  580.8 0.1 reshape.105
  580.9 0.1 reshape.107
  581.0 0.5 broadcast.11
  581.5 0.7 reduce.16
  582.2 0.1 reshape.106
  582.2 0.1 concatenate.7
  582.3 58.3 %all-reduce.1 = f32[16,576]{1,0:T(8,128)S(1)} all-reduce(f32[16,576]{1,0:T(8,128)S(1)} %concatenate.7), channel_id=3, replica_groups=mesh['fsdp'=16,'dp'=2] {'fsdp'}, use_global_device_ids=true, to_apply=%region_0.0.clone | all-reduce | flops 9216 | bytes 73728
  640.7 0.7 constant_dynamic-slice_fusion
  641.3 4.9 psum.35
  646.2 0.6 slice.134
  646.9 0.6 slice_bitcast_fusion.4
  647.5 0.6 slice_bitcast_fusion
  648.1 1.8 convert_element_type.33
  649.9 1.8 convert_element_type.35
  651.7 1.7 convert_element_type.29
  653.4 1.6 convert_element_type.31
  (28 shorter events, 0.3 us)
Async XLA Ops:
  7.2 83.3 %all-gather.6.cloned.1.call-start = ((), (), s32[]{:S(2)}) async-start(), calls=%async_computation.4 | async-start | bytes 3760128 | tf_op jit(solution)/shard_map/all_gather | solution.py:325
  7.9 125.9 %all-gather.8.cloned.1.call-start = ((), (), s32[]{:S(2)}) async-start(), calls=%async_computation.5 | async-start | bytes 1253376 | tf_op jit(solution)/shard_map/all_gather | solution.py:325
  8.7 145.3 %all-gather.10.cloned.1.call-start = ((), (), s32[]{:S(2)}) async-start(), calls=%async_computation.6 | async-start | bytes 5013504 | tf_op jit(solution)/shard_map/all_gather | solution.py:325
  9.4 198.4 %all-gather.12.cloned.1.call-start = ((), (), s32[]{:S(2)}) async-start(), calls=%async_computation.7 | async-start | bytes 5013504 | tf_op jit(solution)/shard_map/all_gather | solution.py:325
  10.0 350.7 %reduce-scatter.7.cloned.1.call-start = ((), (), s32[]{:S(2)}) async-start(), calls=%async_computation.9 | async-start | bytes 1253376 | tf_op jit(solution)/shard_map/reduce_scatter | solution.py:329
  207.8 64.6 %copy-start.4 = (bf16[5,416,768]{2,1,0:T(8,128)(2,1)S(1)}, bf16[5,416,768]{2,1,0:T(8,128)(2,1)}, u32[]{:S(2)}) copy-start(bf16[5,416,768]{2,1,0:T(8,128)(2,1)} %get-tuple-element.30.att_ref.mixed_ref) | copy-start | bytes 9584644
  278.3 127.8 %reduce-scatter.5.cloned.1.call-start = ((), (), s32[]{:S(2)}) async-start(), calls=%async_computation.8 | async-start | bytes 3760128 | tf_op jit(solution)/shard_map/reduce_scatter | solution.py:329
  278.4 32.9 %copy-start.6 = (bf16[5,416,768]{2,1,0:T(8,128)(2,1)S(1)}, bf16[5,416,768]{2,1,0:T(8,128)(2,1)}, u32[]{:S(2)}) copy-start(bf16[5,416,768]{2,1,0:T(8,128)(2,1)} %get-tuple-element.42) | copy-start | bytes 9584644
  324.4 1.9 copy-start.5
  324.5 159.9 %reduce-scatter.9.cloned.1.call-start = ((), (), s32[]{:S(2)}) async-start(), calls=%async_computation.10 | async-start | bytes 5013504 | tf_op jit(solution)/shard_map/reduce_scatter | solution.py:329
  342.5 2.0 copy-start.3
  342.5 220.6 %reduce-scatter.11.cloned.1.call-start = ((), (), s32[]{:S(2)}) async-start(), calls=%async_computation.11 | async-start | bytes 5013504 | tf_op jit(solution)/shard_map/reduce_scatter | solution.py:329
  360.6 287.5 %all-reduce.5.cloned.1.call-start = ((), (), s32[]{:S(2)}) async-start(), calls=%async_computation.12 | async-start | bytes 1769472 | tf_op jit(solution)/shard_map/psum | solution.py:330
  563.1 17.4 %copy-start.2 = (f32[1,1536]{1,0:T(1,128)S(1)}, f32[1,1536]{1,0:T(1,128)}, u32[]{:S(2)}) copy-start(f32[1,1536]{1,0:T(1,128)} %get-tuple-element.39) | copy-start | bytes 18436
  563.1 17.5 %copy-start.1 = (f32[8,768]{1,0:T(8,128)S(1)}, f32[8,768]{1,0:T(8,128)}, u32[]{:S(2)}) copy-start(f32[8,768]{1,0:T(8,128)} %get-tuple-element.40) | copy-start | bytes 73732
  563.1 18.4 %copy-start = (f32[1,3072]{1,0:T(1,128)S(1)}, f32[1,3072]{1,0:T(1,128)}, u32[]{:S(2)}) copy-start(f32[1,3072]{1,0:T(1,128)} %get-tuple-element.41) | copy-start | bytes 36868
Sparse Core Ops, SparseCore 0:
  10.3 50.1 all-gather.5
  62.8 37.0 all-gather.7
  102.1 51.7 all-gather.9
  156.1 51.6 all-gather.11
  278.5 56.7 reduce-scatter.6
  338.9 67.1 reduce-scatter.4
  410.0 74.3 reduce-scatter.8
  488.2 74.7 reduce-scatter.10
  565.6 35.8 all-reduce.4

commit v2 on v1

--- a/solution.py
+++ b/solution.py
@@ -1,3 +1,5 @@
+import functools
+
 import jax
 import jax.numpy as jnp
 from jax import lax
@@ -43,27 +45,28 @@
     return (lane % (2 * HEAD_DIM)) < HEAD_DIM
 
 
-def attn_fwd_kernel(
-    x_ref, segc_ref, segr_ref, w_ref, gain_ref, shift_ref, bias_ref,
-    h1_ref, qkv_ref, p_ref, mixed_ref, kz_ref, vt_ref, mt_ref, mask_ref,
+def attn_fwd_row(
+    x_ref, segc_ref, segr_ref, w_ref, small_ref,
+    h1_ref, qkv_ref, p_ref, mixed_ref, kz_ref, vt_ref, mt_ref, mask_ref, hook,
 ):
     width = x_ref.shape[1]
     heads = width // HEAD_DIM
     xhat, _ = norm_parts(x_ref[...].astype(F32))
-    h1 = (xhat * gain_ref[...] + shift_ref[...]).astype(BF16)
+    h1 = (xhat * small_ref[0:1, :] + small_ref[1:2, :]).astype(BF16)
     h1_ref[...] = h1
     low = half_masks(width)
-    q = (dot(h1, w_ref[:, :width]) + bias_ref[:, :width]).astype(BF16)
+    q = (dot(h1, w_ref[:, :width]) + small_ref[8:9, :]).astype(BF16)
     qkv_ref[:, :width] = q * jnp.asarray(0.125, BF16)
     k = dot(h1, w_ref[:, width : 2 * width]).astype(BF16)
     qkv_ref[:, width : 2 * width] = k
     zero = jnp.zeros_like(k)
     kz_ref[0] = jnp.where(low, k, zero)
     kz_ref[1] = jnp.where(low, zero, k)
-    v = (dot(h1, w_ref[:, 2 * width : 3 * width]) + bias_ref[:, width:]).astype(BF16)
+    v = (dot(h1, w_ref[:, 2 * width :]) + small_ref[9:10, :]).astype(BF16)
     qkv_ref[:, 2 * width :] = v
     vt_ref[...] = v.T
     mask_ref[...] = jnp.where(segc_ref[...] == segr_ref[...], 0.0, -1e30)
+    hook(0)
     for head in range(heads):
         pair = slice(head // 2 * 128, head // 2 * 128 + 128)
         rows = slice(head * HEAD_DIM, (head + 1) * HEAD_DIM)
@@ -73,7 +76,323 @@
         probs = (expo * (1.0 / total)).astype(BF16)
         p_ref[head] = probs
         mt_ref[rows, :] = dot(vt_ref[rows, :], probs)
+        if head in (3, 7):
+            hook(1 + head // 4)
     mixed_ref[...] = mt_ref[...].T.astype(BF16)
+    hook(3)
+
+
+def attn_fwd_kernel(
+    x_ref, segc_ref, segr_ref, w_ref, small_ref,
+    h1_ref, qkv_ref, p_ref, mixed_ref, kz_ref, vt_ref, mt_ref, mask_ref,
+):
+    attn_fwd_row(
+        x_ref, segc_ref, segr_ref, w_ref, small_ref,
+        h1_ref, qkv_ref, p_ref, mixed_ref, kz_ref, vt_ref, mt_ref, mask_ref, lambda point: None,
+    )
+
+
+class Place:
+    def __init__(self):
+        fsdp = lax.axis_index("fsdp")
+        self.fsdp = fsdp
+        self.z = fsdp // 4
+        self.y = (fsdp // 2) % 2
+        self.c = fsdp % 2
+        self.x = lax.axis_index("dp")
+
+    def device(self, z=None, y=None, c=None, x=None):
+        z = self.z if z is None else z
+        y = self.y if y is None else y
+        c = self.c if c is None else c
+        x = self.x if x is None else x
+        return {"fsdp": (z * 2 + y) * 2 + c, "dp": x}
+
+    def greet(self):
+        barrier = pltpu.get_barrier_semaphore()
+
+        def signal(device):
+            pl.semaphore_signal(
+                barrier, inc=1, device_id=device, device_id_type=pl.DeviceIdType.MESH
+            )
+
+        signal(self.device(c=1 - self.c))
+        signal(self.device(y=1 - self.y))
+        signal(self.device(x=1 - self.x))
+
+        @pl.when(self.z > 0)
+        def _():
+            signal(self.device(z=self.z - 1))
+
+        @pl.when(self.z < 3)
+        def _():
+            signal(self.device(z=self.z + 1))
+
+        upper = jnp.where(self.z > 0, 1, 0)
+        lower = jnp.where(self.z < 3, 1, 0)
+        pl.semaphore_wait(barrier, 3 + upper + lower)
+
+
+RELS = [(0, 0)] + [(d, h) for d in range(2) for h in range(1, 4)]
+GATHER_SLOTS = 41
+
+
+class Gather:
+    def __init__(self, place, index, dst, own, send, recv, local):
+        self.place, self.index, self.dst, self.own = place, index, dst, own
+        self.send, self.recv, self.local = send, recv, local
+        self.rows, self.cols = own.shape
+
+    def source_z(self, rel):
+        d, h = rel
+        return self.place.z - h if d == 0 else self.place.z + h
+
+    def exists(self, rel):
+        d, h = rel
+        if h == 0:
+            return None
+        return self.place.z >= h if d == 0 else self.place.z + h <= 3
+
+    def guard(self, rel, body):
+        cond = self.exists(rel)
+        if cond is None:
+            body()
+        else:
+            pl.when(cond)(body)
+
+    def view(self, ref, start, half):
+        if half is None:
+            return ref.at[pl.ds(start, self.rows), :]
+        width = self.cols // 2
+        first = pl.multiple_of(half * width, 128)
+        return ref.at[pl.ds(start, self.rows), pl.ds(first, width)]
+
+    def copy(self, slot, rel, y, c, half, device, own=False):
+        index = (self.source_z(rel) * 2 + y) * 2 + c
+        start = pl.multiple_of(index * self.rows, self.rows)
+        view = self.view(self.dst, start, half)
+        src = self.view(self.own, 0, half) if own else view
+        return pltpu.make_async_remote_copy(
+            src_ref=src,
+            dst_ref=view,
+            send_sem=self.send.at[self.index, slot],
+            recv_sem=self.recv.at[self.index, slot],
+            device_id=device,
+            device_id_type=pl.DeviceIdType.MESH,
+        )
+
+    def z_copy(self, d, rel, own=False):
+        place = self.place
+        target = place.z + 1 if d == 0 else place.z - 1
+        return self.copy(
+            d * 3 + rel[1], rel, place.y, place.c, None, place.device(z=target), own
+        )
+
+    def z_room(self, d):
+        return self.place.z < 3 if d == 0 else self.place.z > 0
+
+    def y_copy(self, rel, own=False):
+        place = self.place
+        return self.copy(
+            6 + RELS.index(rel), rel, place.y, place.c, place.x, place.device(y=1 - place.y), own
+        )
+
+    def x_copy(self, rel):
+        place = self.place
+        return self.copy(
+            13 + RELS.index(rel), rel, 1 - place.y, place.c, place.x, place.device(x=1 - place.x)
+        )
+
+    def c_copy(self, rel, own=False):
+        place = self.place
+        return self.copy(
+            20 + RELS.index(rel), rel, place.y, place.c, None, place.device(c=1 - place.c), own
+        )
+
+    def cy_copy(self, rel, k):
+        place = self.place
+        half = place.x if k == 0 else 1 - place.x
+        return self.copy(
+            27 + 2 * RELS.index(rel) + k, rel, 1 - place.y, place.c, half,
+            place.device(c=1 - place.c),
+        )
+
+    def local_copy(self):
+        start = pl.multiple_of(self.place.fsdp * self.rows, self.rows)
+        return pltpu.make_async_copy(
+            self.own, self.dst.at[pl.ds(start, self.rows), :], self.local.at[self.index]
+        )
+
+    def begin(self):
+        own = (0, 0)
+        for d in range(2):
+            pl.when(self.z_room(d))(lambda d=d: self.z_copy(d, own, True).start())
+        self.y_copy(own, True).start()
+        self.c_copy(own, True).start()
+        self.local_copy().start()
+
+    def arrived(self, slot, rel, y, c, half):
+        self.copy(slot, rel, y, c, half, self.place.device()).wait_recv()
+
+    def on_z(self, rel):
+        d, h = rel
+
+        def body():
+            place = self.place
+            self.arrived(d * 3 + h - 1, rel, place.y, place.c, None)
+            if h < 3:
+                pl.when(self.z_room(d))(lambda: self.z_copy(d, rel).start())
+            self.y_copy(rel).start()
+            self.c_copy(rel).start()
+
+        self.guard(rel, body)
+
+    def on_y(self, rel):
+        def body():
+            place = self.place
+            self.arrived(6 + RELS.index(rel), rel, 1 - place.y, place.c, place.x)
+            self.x_copy(rel).start()
+            self.cy_copy(rel, 0).start()
+
+        self.guard(rel, body)
+
+    def on_x(self, rel):
+        def body():
+            place = self.place
+            self.arrived(13 + RELS.index(rel), rel, 1 - place.y, place.c, 1 - place.x)
+            self.cy_copy(rel, 1).start()
+
+        self.guard(rel, body)
+
+    def events(self):
+        up, down = [(0, h) for h in range(1, 4)], [(1, h) for h in range(1, 4)]
+        own = (0, 0)
+        return [
+            lambda: (self.on_z(up[0]), self.on_z(down[0])),
+            lambda: self.on_y(own),
+            lambda: (self.on_z(up[1]), self.on_z(down[1])),
+            lambda: (self.on_y(up[0]), self.on_y(down[0])),
+            lambda: self.on_x(own),
+            lambda: (self.on_z(up[2]), self.on_z(down[2])),
+            lambda: (self.on_y(up[1]), self.on_y(down[1])),
+            lambda: (self.on_x(up[0]), self.on_x(down[0])),
+            lambda: (self.on_y(up[2]), self.on_y(down[2])),
+            lambda: (self.on_x(up[1]), self.on_x(down[1])),
+            lambda: (self.on_x(up[2]), self.on_x(down[2])),
+        ]
+
+    def finish_recv(self):
+        place = self.place
+        self.local_copy().wait()
+        for rel in RELS:
+
+            def body(rel=rel):
+                number = RELS.index(rel)
+                self.arrived(20 + number, rel, place.y, 1 - place.c, None)
+                self.arrived(27 + 2 * number, rel, 1 - place.y, 1 - place.c, place.x)
+                self.arrived(28 + 2 * number, rel, 1 - place.y, 1 - place.c, 1 - place.x)
+
+            self.guard(rel, body)
+
+    def finish_send(self):
+        for rel in RELS:
+
+            def body(rel=rel):
+                d, h = rel
+                for way in range(2) if h == 0 else (d,):
+                    if h < 3:
+                        pl.when(self.z_room(way))(
+                            lambda way=way: self.z_copy(way, rel).wait_send()
+                        )
+                self.y_copy(rel).wait_send()
+                self.x_copy(rel).wait_send()
+                self.c_copy(rel).wait_send()
+                self.cy_copy(rel, 0).wait_send()
+                self.cy_copy(rel, 1).wait_send()
+
+            self.guard(rel, body)
+
+
+def place_small(one_ref, two_ref, four_ref, shard, fsdp):
+    width = one_ref.shape[1]
+    per_row = width // shard
+    rows = lax.broadcasted_iota(jnp.int32, (8, width), 0)
+    ones = pltpu.roll(one_ref[...], fsdp * shard, 1)
+    two = pltpu.roll(two_ref[...], (fsdp * 2 % per_row) * shard, 1)
+    four = pltpu.roll(four_ref[...], (fsdp * 4 % per_row) * shard, 1)
+    two = jnp.where(rows == fsdp * 2 // per_row, two, 0.0)
+    four = jnp.where(rows == 2 + fsdp * 4 // per_row, four, 0.0)
+    return jnp.concatenate([ones, two + four], axis=0)
+
+
+def gather_attn_kernel(
+    x_ref, segc_ref, segr_ref, one_ref, two_ref, four_ref,
+    qkv_own, out_own, up_own, down_own,
+    h1_ref, qkv_ref, p_ref, mixed_ref, small_ref, wq_hbm, out_hbm, up_hbm, down_hbm,
+    wq_ref, tiny_own, tiny_ref, kz_ref, vt_ref, mt_ref, mask_ref, send, recv, local,
+):
+    place = Place()
+    row = pl.program_id(0)
+    last = pl.num_programs(0) - 1
+    parts = wq_ref.shape[0] // qkv_own.shape[0]
+    tiny = Gather(place, 0, tiny_ref, tiny_own, send, recv, local)
+    first = Gather(place, 1, wq_ref, qkv_own, send, recv, local)
+    rest = [
+        Gather(place, 2 + i, dst, own, send, recv, local)
+        for i, (dst, own) in enumerate(
+            ((up_hbm, up_own), (down_hbm, down_own), (out_hbm, out_own))
+        )
+    ]
+    keep = pltpu.make_async_copy(wq_ref, wq_hbm, local.at[5])
+
+    @pl.when(row == 0)
+    def _():
+        tiny_own[...] = place_small(one_ref, two_ref, four_ref, qkv_own.shape[0], place.fsdp).astype(BF16)
+        place.greet()
+        tiny.begin()
+        first.begin()
+        early, main = tiny.events(), first.events()
+        for step in range(len(main)):
+            early[step]()
+            main[step]()
+            if step == 5:
+                for item in rest:
+                    item.begin()
+        tiny.finish_recv()
+        total = tiny_ref[0:16, :].astype(F32)
+        for index in range(1, parts):
+            total += tiny_ref[16 * index : 16 * index + 16, :].astype(F32)
+        small_ref[...] = total
+        first.finish_recv()
+        keep.start()
+
+    queue = [event for item in rest for event in item.events()]
+    points = 4 * 5 - 1
+    share = -(-len(queue) // points)
+
+    def hook(point):
+        for r in range(5):
+            number = r * 4 + point
+            todo = queue[number * share : (number + 1) * share]
+            if todo:
+
+                @pl.when(row == r)
+                def _(todo=todo):
+                    for event in todo:
+                        event()
+
+    attn_fwd_row(
+        x_ref, segc_ref, segr_ref, wq_ref, small_ref,
+        h1_ref, qkv_ref, p_ref, mixed_ref, kz_ref, vt_ref, mt_ref, mask_ref, hook,
+    )
+
+    @pl.when(row == last)
+    def _():
+        keep.wait()
+        for item in rest:
+            item.finish_recv()
+        for item in [tiny, first] + rest:
+            item.finish_send()
 
 
 def attn_bwd_kernel(
@@ -118,18 +437,18 @@
 
 
 def mlp_kernel(
-    x_ref, att_ref, dy_ref, wo_ref, wu_ref, wd_ref, bo_ref, gain_ref, shift_ref, bu_ref, bd_ref,
+    x_ref, att_ref, dy_ref, wo_ref, wu_ref, wd_ref, small_ref,
     out_ref, h2_ref, act_ref, dpre_ref, dz_ref, datt_ref, dsmall_ref, dbu_ref,
 ):
     width = x_ref.shape[1]
     hidden = wu_ref.shape[1]
-    chunk = 512 if hidden % 512 == 0 else 128
-    middle = x_ref[...].astype(F32) + dot(att_ref[...], wo_ref[...]) + bo_ref[...]
+    gain, shift = small_ref[3:4, :], small_ref[4:5, :]
+    middle = x_ref[...].astype(F32) + dot(att_ref[...], wo_ref[...]) + small_ref[2:3, :]
     xhat, inv = norm_parts(middle)
-    h2 = (xhat * gain_ref[...] + shift_ref[...]).astype(BF16)
+    h2 = (xhat * gain + shift).astype(BF16)
     h2_ref[...] = h2
     dy = dy_ref[...]
-    out = middle + bd_ref[...]
+    out = middle + small_ref[5:6, :]
     dh2 = None
 
     @pl.when(pl.program_id(0) == 0)
@@ -137,9 +456,9 @@
         dsmall_ref[...] = jnp.zeros_like(dsmall_ref)
         dbu_ref[...] = jnp.zeros_like(dbu_ref)
 
-    for start in range(0, hidden, chunk):
-        cols = slice(start, start + chunk)
-        pre = dot(h2, wu_ref[:, cols]) + bu_ref[:, cols]
+    for part_index in range(hidden // width):
+        cols = slice(part_index * width, (part_index + 1) * width)
+        pre = dot(h2, wu_ref[:, cols]) + small_ref[10 + part_index : 11 + part_index, :]
         dact = dot_nt(dy, wd_ref[cols, :])
         cdf = 0.5 * (1.0 + lax.erf(pre * 0.7071067811865476))
         pdf = jnp.exp(-0.5 * pre * pre) * 0.3989422804014327
@@ -154,7 +473,7 @@
         dh2 = part if dh2 is None else dh2 + part
     out_ref[...] = out.astype(BF16)
     wide_dy = dy.astype(F32)
-    dmiddle = wide_dy + norm_grad(xhat, inv, dh2, gain_ref[...])
+    dmiddle = wide_dy + norm_grad(xhat, inv, dh2, gain)
     dz = dmiddle.astype(BF16)
     dz_ref[...] = dz
     datt_ref[...] = dot_nt(dz, wo_ref[...]).astype(BF16)
@@ -164,11 +483,11 @@
     dsmall_ref[3:4, :] += jnp.sum(wide_dy, axis=0, keepdims=True)
 
 
-def input_grad_kernel(x_ref, dproj_ref, dz_ref, w_ref, gain_ref, dx_ref, dsmall_ref):
+def input_grad_kernel(x_ref, dproj_ref, dz_ref, w_ref, small_ref, dx_ref, dsmall_ref):
     width = x_ref.shape[1]
     dh1 = dot_nt(dproj_ref[...], w_ref[:, : 3 * width])
     xhat, inv = norm_parts(x_ref[...].astype(F32))
-    dx = dz_ref[...].astype(F32) + norm_grad(xhat, inv, dh1, gain_ref[...])
+    dx = dz_ref[...].astype(F32) + norm_grad(xhat, inv, dh1, small_ref[0:1, :])
     dx_ref[...] = dx.astype(BF16)
 
     @pl.when(pl.program_id(0) == 0)
@@ -195,7 +514,7 @@
     return jax.ShapeDtypeStruct(shape, dtype)
 
 
-def run(kernel, grid, in_specs, outs, out_specs, scratch, args, flops, name):
+def run(kernel, grid, in_specs, outs, out_specs, scratch, args, flops, name, collective_id=None):
     total = sum(a.size * a.dtype.itemsize for a in args)
     total += sum(o.size * jnp.dtype(o.dtype).itemsize for o in outs)
     return pl.pallas_call(
@@ -206,50 +525,91 @@
         out_shape=outs,
         scratch_shapes=scratch,
         compiler_params=pltpu.CompilerParams(
-            dimension_semantics=("arbitrary",), vmem_limit_bytes=VMEM_LIMIT
+            dimension_semantics=("arbitrary",),
+            vmem_limit_bytes=VMEM_LIMIT,
+            collective_id=collective_id,
+            has_side_effects=collective_id is not None,
         ),
         cost_estimate=pl.CostEstimate(flops=flops, bytes_accessed=total, transcendentals=0),
         name=name,
     )(*args)
 
 
-def attn_fwd(x, segs, w, gain, shift, bias):
-    rows, slots, width = x.shape
-    heads = width // HEAD_DIM
+def attn_outs(rows, slots, width, heads):
     outs = (
         sds((rows, slots, width), BF16),
         sds((rows, slots, 3 * width), BF16),
         sds((rows, heads, slots, slots), BF16),
         sds((rows, slots, width), BF16),
     )
+    specs = [
+        row_spec(slots, width),
+        row_spec(slots, 3 * width),
+        row_spec(heads, slots, slots),
+        row_spec(slots, width),
+    ]
+    scratch = [
+        pltpu.VMEM((2, slots, width), BF16),
+        pltpu.VMEM((width, slots), BF16),
+        pltpu.VMEM((width, slots), F32),
+        pltpu.VMEM((slots, slots), F32),
+    ]
+    return outs, specs, scratch
+
+
+def attn_flops(rows, slots, width):
+    return rows * (6 * slots * width * width + 4 * slots * slots * width * 4)
+
+
+def attn_fwd(x, segs, w, small):
+    rows, slots, width = x.shape
+    outs, specs, scratch = attn_outs(rows, slots, width, width // HEAD_DIM)
     return run(
         attn_fwd_kernel,
         (rows,),
         [
-            row_spec(slots, width),
-            row_spec(slots, 1),
-            row_spec(1, slots),
-            whole(width, 3 * width),
-            whole(1, width),
-            whole(1, width),
-            whole(1, 2 * width),
+            row_spec(slots, width), row_spec(slots, 1), row_spec(1, slots),
+            whole(width, 3 * width), whole(16, width),
         ],
         outs,
+        specs,
+        scratch,
+        (x, segs[:, :, None], segs[:, None, :], w, small),
+        attn_flops(rows, slots, width),
+        "attn_fwd",
+    )
+
+
+def gather_attn(x, segs, smalls, qkv_own, out_own, up_own, down_own):
+    rows, slots, width = x.shape
+    parts = width // qkv_own.shape[0]
+    hidden = up_own.shape[1]
+    outs, specs, scratch = attn_outs(rows, slots, width, width // HEAD_DIM)
+    hbm = pl.BlockSpec(memory_space=pl.ANY)
+    return run(
+        gather_attn_kernel,
+        (rows,),
+        [row_spec(slots, width), row_spec(slots, 1), row_spec(1, slots)]
+        + [whole(8, width)] * 3
+        + [whole(*own.shape) for own in (qkv_own, out_own, up_own, down_own)],
+        outs + (
+            sds((16, width), F32), sds((width, 3 * width), BF16), sds((width, width), BF16),
+            sds((width, hidden), BF16), sds((hidden, width), BF16),
+        ),
+        specs + [acc_spec(16, width), hbm, hbm, hbm, hbm],
         [
-            row_spec(slots, width),
-            row_spec(slots, 3 * width),
-            row_spec(heads, slots, slots),
-            row_spec(slots, width),
+            pltpu.VMEM((width, 3 * width), BF16),
+            pltpu.VMEM((16, width), BF16),
+            pltpu.VMEM((16 * parts, width), BF16),
+        ] + scratch + [
+            pltpu.SemaphoreType.DMA((5, GATHER_SLOTS)),
+            pltpu.SemaphoreType.DMA((5, GATHER_SLOTS)),
+            pltpu.SemaphoreType.DMA((6,)),
         ],
-        [
-            pltpu.VMEM((2, slots, width), BF16),
-            pltpu.VMEM((width, slots), BF16),
-            pltpu.VMEM((width, slots), F32),
-            pltpu.VMEM((slots, slots), F32),
-        ],
-        (x, segs[:, :, None], segs[:, None, :], w, gain, shift, bias),
-        rows * (6 * slots * width * width + 4 * slots * slots * width * 4),
-        "attn_fwd",
+        (x, segs[:, :, None], segs[:, None, :], *smalls, qkv_own, out_own, up_own, down_own),
+        attn_flops(rows, slots, width),
+        "gather_attn",
+        collective_id=0,
     )
 
 
@@ -279,7 +639,7 @@
     )
 
 
-def mlp(x, mixed, dy, wo, wu, wd, bo, gain, shift, bu, bd):
+def mlp(x, mixed, dy, wo, wu, wd, small):
     rows, slots, width = x.shape
     hidden = wu.shape[1]
     act = row_spec(slots, width)
@@ -290,7 +650,7 @@
         [
             act, act, act,
             whole(width, width), whole(width, hidden), whole(hidden, width),
-            whole(1, width), whole(1, width), whole(1, width), whole(1, hidden), whole(1, width),
+            whole(16, width),
         ],
         (
             sds(x.shape, BF16), sds(x.shape, BF16), sds((rows, slots, hidden), BF16),
@@ -299,23 +659,23 @@
         ),
         [act, act, wide, wide, act, act, acc_spec(8, width), acc_spec(1, hidden)],
         [],
-        (x, mixed, dy, wo, wu, wd, bo, gain, shift, bu, bd),
+        (x, mixed, dy, wo, wu, wd, small),
         rows * slots * width * (8 * hidden + 4 * width),
         "mlp",
     )
 
 
-def input_grad(x, dproj, dz, w, gain):
+def input_grad(x, dproj, dz, w, small):
     rows, slots, width = x.shape
     act = row_spec(slots, width)
     return run(
         input_grad_kernel,
         (rows,),
-        [act, row_spec(slots, 3 * width), act, whole(width, 3 * width), whole(1, width)],
+        [act, row_spec(slots, 3 * width), act, whole(width, 3 * width), whole(16, width)],
         (sds(x.shape, BF16), sds((8, width), F32)),
         [act, acc_spec(8, width)],
         [],
-        (x, dproj, dz, w, gain),
+        (x, dproj, dz, w, small),
         rows * slots * width * width * 6,
         "input_grad",
     )
@@ -337,40 +697,45 @@
 
 
 def per_device(
-    block_input, segment_ids, ln1_gain, ln1_bias, qkv_weight, qv_bias, out_weight, out_bias,
+    linked, block_input, segment_ids, ln1_gain, ln1_bias, qkv_weight, qv_bias, out_weight, out_bias,
     ln2_gain, ln2_bias, up_weight, up_bias, down_weight, down_bias, out_cotangent,
 ):
     rows, slots, width = block_input.shape
     shard = ln1_gain.shape[0]
     parts = width // shard
-    small = jnp.concatenate(
-        [
-            ln1_gain, ln1_bias, qv_bias, out_bias, ln2_gain, ln2_bias, up_bias, down_bias,
-        ]
-    )[None]
     sizes = [shard, shard, 2 * shard, shard, shard, shard, 4 * shard, shard]
-    small_full = gather(small).astype(F32)
-    vectors, start = [], 0
-    for size in sizes:
-        vectors.append(small_full[:, start : start + size].reshape(1, size * parts))
-        start += size
-    gain1, shift1, bias_qv, bias_out, gain2, shift2, bias_up, bias_down = vectors
-    w_qkv = gather(qkv_weight)
-    w_out = gather(out_weight)
-    w_up = gather(up_weight)
-    w_down = gather(down_weight)
-
-    h1, qkv, probs, mixed = attn_fwd(block_input, segment_ids, w_qkv, gain1, shift1, bias_qv)
+    ones = [ln1_gain, ln1_bias, out_bias, ln2_gain, ln2_bias, down_bias]
+    if linked:
+
+        def rows_of(vectors):
+            padded = [jnp.pad(v.astype(F32), (0, width - v.shape[0])) for v in vectors]
+            return jnp.stack(padded + [jnp.zeros((width,), F32)] * (8 - len(padded)))
+
+        smalls = (rows_of(ones), rows_of([qv_bias] * 8), rows_of([up_bias] * 8))
+        h1, qkv, probs, mixed, small, w_qkv, w_out, w_up, w_down = gather_attn(
+            block_input, segment_ids, smalls, qkv_weight, out_weight, up_weight, down_weight
+        )
+    else:
+        small = jnp.concatenate(
+            [gather(v)[None] for v in ones]
+            + [jnp.zeros((2, width), BF16)]
+            + [gather(v).reshape(-1, width) for v in (qv_bias, up_bias)]
+            + [jnp.zeros((2, width), BF16)]
+        ).astype(F32)
+        w_qkv = gather(qkv_weight)
+        w_out = gather(out_weight)
+        w_up = gather(up_weight)
+        w_down = gather(down_weight)
+        h1, qkv, probs, mixed = attn_fwd(block_input, segment_ids, w_qkv, small)
     out, h2, act, dpre, dz, dmixed, dsmall2, dbias_up = mlp(
-        block_input, mixed, out_cotangent, w_out, w_up, w_down,
-        bias_out, gain2, shift2, bias_up, bias_down,
+        block_input, mixed, out_cotangent, w_out, w_up, w_down, small
     )
     down_grad = scatter(weight_grad(act, out_cotangent))
     up_grad = scatter(weight_grad(h2, dpre))
     out_grad = scatter(weight_grad(mixed, dz))
     dproj, dbias_qv = attn_bwd(qkv, probs, mixed, dmixed)
     qkv_grad = scatter(weight_grad(h1, dproj))
-    dx, dsmall1 = input_grad(block_input, dproj, dz, w_qkv, gain1)
+    dx, dsmall1 = input_grad(block_input, dproj, dz, w_qkv, small)
     grads = [
         dsmall1[0:1], dsmall1[1:2], dbias_qv, dsmall2[0:1],
         dsmall2[1:2], dsmall2[2:3], dbias_up, dsmall2[3:4],
@@ -390,9 +755,10 @@
 
 def solution(mesh):
     both = ("fsdp", "dp")
+    linked = mesh.shape["fsdp"] == 16 and mesh.shape["dp"] == 2
     vec, mat, act = P("fsdp"), P("fsdp", None), P(both, None, None)
     return jax.shard_map(
-        per_device,
+        functools.partial(per_device, linked),
         mesh=mesh,
         in_specs=(
             act, P(both, None), vec, vec, mat, vec, mat, vec, vec, vec, mat, vec, mat, vec, act,

time: 669 us -> 588 us (0.88)
  waiting for transfers between devices: 279 us -> 204 us
  blocking collectives: 127 us -> 63.2 us
  Pallas kernels: 157 us -> 220 us
  local copies, waits for them, and re-layouts: 24.4 us -> 14.1 us
    all_gather x4 -> x0, waiting for transfers between devices: 74 us -> none  [gather(): return lax.all_gather(shard, 'fsdp', axis=0, tiled=True)]
    unnamed x2 -> x1, blocking collectives: 122 us -> 58.3 us
    pallas_call x4, Pallas kernels: 157 us -> 220 us  [run(): pl.pallas_call(kernel, grid=grid, in_specs=in_specs, out_specs=out_specs,...]
  transfers between devices with their start and end apart: 9 -> 5, of which waited for: 5 -> 3; matrix products, arithmetic and copies ran while one was open for 10% -> 9% of each run, Pallas kernels for 14% -> 9%
where the time goes in v2:
time: 588 us; the launch traced here: 579 us
  Pallas kernels  220 us (37%)
  waiting for transfers between devices  204 us (35%)
  blocking collectives  63.2 us (11%)
  matrix products  51 us (9%)
  between operations  14.2 us (2%)
  local copies, waits for them, and re-layouts  14.1 us (2%)
  other arithmetic  12.9 us (2%)
    pallas_call x4, Pallas kernels, run(): pl.pallas_call(kernel, grid=grid, in_specs=in_specs, out_specs=out_specs,...  220 us
    reduce_scatter x4, waiting for transfers between devices, scatter(): owned = lax.psum_scatter(full, 'fsdp', scatter_dimension=0, tiled=True)  204 us
    unnamed x1, blocking collectives  58.3 us
    dot_general x4, matrix products, dot_tn(): return lax.dot_general(left, right, TN, preferred_element_type=F32)  51 us
  transfers between devices with their start and end apart: 5, of which 3 were waited for; matrix products, arithmetic and copies ran while one was open for 9% of the time, Pallas kernels for 9%

profile of v2, /device:TPU:0, one launch (start us, length us, event | category | flops | bytes accessed | tf_op | source)
XLA Modules:
  0.0 579.0 jit_solution(9996292690912358836)
XLA Ops:
  7.2 0.0 reduce-scatter.7.cloned.1.call-start
  7.2 1.3 broadcast_in_dim.7.segr_ref
  8.6 2.1 copy.30.segc_ref
  10.6 0.7 pad_convert_fusion.7
  11.3 0.7 pad_convert_fusion.6
  12.0 0.7 pad_convert_fusion.5
  12.6 0.7 pad_convert_fusion.4
  13.3 0.7 pad_convert_fusion.3
  13.9 0.7 pad_convert_fusion.2
  14.6 0.7 pad_convert_fusion.1
  15.3 0.7 pad_convert_fusion
  15.9 0.6 stack.77.one_ref
  16.6 0.6 stack.78.two_ref
  17.2 0.6 stack.79.four_ref
  17.8 108.4 %gather_attn.1 = (bf16[5,416,768]{2,1,0:T(8,128)(2,1)}, bf16[5,416,2304]{2,1,0:T(8,128)(2,1)}, bf16[5,12,416,416]{3,2,1,0:T(8,128)(2,1)}, bf16[5,416,768]{2,1,0:...) custom-call(bf16[5,416,768]{2,1,0:T(8,128)(2,1)} %x_ref.5, ...), custom_call_target="tpu_custom_call" | custom-call | flops 17993564160 | bytes 55116032 | tf_op jit(solution)/shard_map/gather_attn/pallas_call | solution.py:520
  126.2 61.8 %mlp.1 = (bf16[5,416,768]{2,1,0:T(8,128)(2,1)}, bf16[5,416,768]{2,1,0:T(8,128)(2,1)}, bf16[5,416,3072]{2,1,0:T(8,128)(2,1)}, bf16[5,416,3072]{2,1,0:T(8,128)(2,1...) custom-call(bf16[5,416,768]{2,1,0:T(8,128)(2,1)} %x_ref.5, ...), custom_call_target="tpu_custom_call" | custom-call | flops 44166021120 | bytes 58626048 | tf_op jit(solution)/shard_map/mlp/pallas_call | solution.py:520
  188.1 5.9 %bitcast_convert_fusion.3 = bf16[768,768]{1,0:T(8,128)(2,1)} fusion(bf16[5,416,768]{2,1,0:T(8,128)(2,1)S(1)} %copy-done.5, bf16[5,416,768]{2,1,0:T(8,128)(2,1)} %get-tuple-element.45.dz_ref), kind=kOutput, calls=%fused_computation.3 | convolution fusion | flops 2454257664 | bytes 7569408 | tf_op jit(solution)/shard_map/dot_general | solution.py:27
  194.0 0.0 reduce-scatter.7.cloned.1.call-update
  194.0 0.0 reduce-scatter.5.cloned.1.call-start
  194.1 33.0 %attn_bwd.1 = (bf16[5,416,2304]{2,1,0:T(8,128)(2,1)}, f32[1,1536]{1,0:T(1,128)}) custom-call(bf16[5,416,2304]{2,1,0:T(8,128)(2,1)} %get-tuple-element.41.qkv_ref, bf16[5,12,416,416]{3,2,1,0:T(8,128)(2,1)} %get-tuple-element.42.p_ref, bf16[5,416,768]{2,1,0:T(8,128)(2,1)} %get-tuple-element.35.att_ref.mixed_ref, bf16[5,416,768]{2,1,0:T(8,128)(2,1)} %get-tuple-element.43.do_ref), custom_call_target="tpu_custom_call" | custom-call | flops 21265121280 | bytes 46331904 | tf_op jit(solution)/shard_map/attn_bwd/pallas_call | solution.py:520
  227.1 13.2 %bitcast_convert_fusion.2 = bf16[768,2304]{1,0:T(8,128)(2,1)} fusion(bf16[5,416,768]{2,1,0:T(8,128)(2,1)S(1)} %copy-done.7, bf16[5,416,2304]{2,1,0:T(8,128)(2,1)} %get-tuple-element.44.dproj_ref), kind=kOutput, calls=%fused_computation.2 | convolution fusion | flops 7362772992 | bytes 16318464 | tf_op jit(solution)/shard_map/dot_general | solution.py:27
  240.3 0.0 reduce-scatter.5.cloned.1.call-update
  240.3 0.0 reduce-scatter.9.cloned.1.call-start
  240.3 1.8 copy-done.6
  242.2 15.9 %bitcast_convert_fusion.1 = bf16[768,3072]{1,0:T(8,128)(2,1)} fusion(bf16[5,416,768]{2,1,0:T(8,128)(2,1)S(1)} %copy-done.6, bf16[5,416,3072]{2,1,0:T(8,128)(2,1)} %get-tuple-element.54), kind=kOutput, calls=%fused_computation.1 | convolution fusion | flops 9817030656 | bytes 20692992 | tf_op jit(solution)/shard_map/dot_general | solution.py:27
  258.1 0.0 reduce-scatter.9.cloned.1.call-update
  258.1 0.0 reduce-scatter.11.cloned.1.call-start
  258.2 1.8 copy-done.3
  260.0 16.0 %bitcast_convert_fusion = bf16[3072,768]{1,0:T(8,128)(2,1)} fusion(bf16[5,416,3072]{2,1,0:T(8,128)(2,1)} %get-tuple-element.55, bf16[5,416,768]{2,1,0:T(8,128)(2,1)S(1)} %copy-done.3), kind=kOutput, calls=%fused_computation | convolution fusion | flops 9817030656 | bytes 20692992 | tf_op jit(solution)/shard_map/dot_general | solution.py:27
  276.0 0.0 reduce-scatter.11.cloned.1.call-update
  276.0 0.0 all-reduce.12.cloned.1.call-start
  276.1 0.0 reduce-scatter.7.cloned.1.call-done
  276.1 46.7 %reduce-scatter.5.cloned.1.call-done = bf16[48,2304]{1,0:T(8,128)(2,1)} async-done(((bf16[768,2304]{1,0:T(8,128)(2,1)}), bf16[48,2304]{1,0:T(8,128)(2,1)}) %reduce-scatter.5.cloned.1.call-update) | async-done | bytes 221200 | tf_op jit(solution)/shard_map/reduce_scatter | solution.py:689
  322.8 78.3 %reduce-scatter.9.cloned.1.call-done = bf16[48,3072]{1,0:T(8,128)(2,1)} async-done(((bf16[768,3072]{1,0:T(8,128)(2,1)}), bf16[48,3072]{1,0:T(8,128)(2,1)}) %reduce-scatter.9.cloned.1.call-update) | async-done | bytes 294928 | tf_op jit(solution)/shard_map/reduce_scatter | solution.py:689
  401.1 78.5 %reduce-scatter.11.cloned.1.call-done = bf16[192,768]{1,0:T(8,128)(2,1)} async-done(((bf16[3072,768]{1,0:T(8,128)(2,1)}), bf16[192,768]{1,0:T(8,128)(2,1)}) %reduce-scatter.11.cloned.1.call-update) | async-done | bytes 294928 | tf_op jit(solution)/shard_map/reduce_scatter | solution.py:689
  479.6 0.0 all-reduce.12.cloned.1.call-update
  479.6 0.0 copy-start.2
  479.6 0.0 copy-start.1
  479.6 0.0 copy-start
  479.6 0.0 copy-start.4
  479.6 16.5 %input_grad.1 = (bf16[5,416,768]{2,1,0:T(8,128)(2,1)}, f32[8,768]{1,0:T(8,128)}) custom-call(bf16[5,416,768]{2,1,0:T(8,128)(2,1)} %x_ref.5, bf16[5,416,2304]{2,1,0:T(8,128)(2,1)} %get-tuple-element.44.dproj_ref, bf16[5,416,768]{2,1,0:T(8,128)(2,1)} %get-tuple-element.45.dz_ref, bf16[768,2304]{1,0:T(8,128)(2,1)} %get-tuple-element.46.w_ref, ...), custom_call_target="tpu_custom_call" | custom-call | flops 7361003520 | bytes 22781952 | tf_op jit(solution)/shard_map/input_grad/pallas_call | solution.py:520
  496.2 0.8 slice_reduce_fusion.4
  497.0 0.1 reshape.72
  497.1 0.1 reshape.73
  497.2 0.1 reshape.74
  497.3 0.1 reshape.75
  497.4 0.1 reshape.76
  497.4 0.1 reshape.77
  497.5 0.1 reshape.79
  497.6 0.5 broadcast.30
  498.1 0.7 reduce.16
  498.8 0.1 reshape.78
  498.9 0.6 dynamic-slice
  499.5 0.1 concatenate.3
  499.6 58.3 %all-reduce.8 = f32[16,576]{1,0:T(8,128)S(1)} all-reduce(f32[16,576]{1,0:T(8,128)S(1)} %concatenate.3), channel_id=2, replica_groups=mesh['fsdp'=16,'dp'=2] {'fsdp'}, use_global_device_ids=true, to_apply=%region_0.1.clone | all-reduce | flops 9216 | bytes 73728
  557.8 0.7 constant_dynamic-slice_fusion
  558.5 4.9 psum.35
  563.4 0.6 slice.94
  564.1 0.6 slice_bitcast_fusion.4
  564.6 0.6 slice_bitcast_fusion
  565.3 1.8 convert_element_type.76
  567.1 1.8 convert_element_type.78
  568.9 1.7 convert_element_type.72
  570.6 1.6 convert_element_type.74
  (20 shorter events, 0.1 us)
Async XLA Ops:
  7.2 268.9 %reduce-scatter.7.cloned.1.call-start = ((), (), s32[]{:S(2)}) async-start(), calls=%async_computation.5 | async-start | bytes 1253376 | tf_op jit(solution)/shard_map/reduce_scatter | solution.py:689
  126.2 61.8 %copy-start.5 = (bf16[5,416,768]{2,1,0:T(8,128)(2,1)S(1)}, bf16[5,416,768]{2,1,0:T(8,128)(2,1)}, u32[]{:S(2)}) copy-start(bf16[5,416,768]{2,1,0:T(8,128)(2,1)} %get-tuple-element.35.att_ref.mixed_ref) | copy-start | bytes 9584644
  194.0 128.8 %reduce-scatter.5.cloned.1.call-start = ((), (), s32[]{:S(2)}) async-start(), calls=%async_computation.4 | async-start | bytes 3760128 | tf_op jit(solution)/shard_map/reduce_scatter | solution.py:689
  194.1 33.0 %copy-start.7 = (bf16[5,416,768]{2,1,0:T(8,128)(2,1)S(1)}, bf16[5,416,768]{2,1,0:T(8,128)(2,1)}, u32[]{:S(2)}) copy-start(bf16[5,416,768]{2,1,0:T(8,128)(2,1)} %get-tuple-element.52) | copy-start | bytes 9584644
  240.3 1.9 copy-start.6
  240.3 160.8 %reduce-scatter.9.cloned.1.call-start = ((), (), s32[]{:S(2)}) async-start(), calls=%async_computation.6 | async-start | bytes 5013504 | tf_op jit(solution)/shard_map/reduce_scatter | solution.py:689
  258.1 1.9 copy-start.3
  258.1 221.5 %reduce-scatter.11.cloned.1.call-start = ((), (), s32[]{:S(2)}) async-start(), calls=%async_computation.7 | async-start | bytes 5013504 | tf_op jit(solution)/shard_map/reduce_scatter | solution.py:689
  276.0 289.2 %all-reduce.12.cloned.1.call-start = ((), (), s32[]{:S(2)}) async-start(), calls=%async_computation.8 | async-start | bytes 1769472 | tf_op jit(solution)/shard_map/psum | solution.py:690
  479.6 17.5 %copy-start.2 = (f32[1,1536]{1,0:T(1,128)S(1)}, f32[1,1536]{1,0:T(1,128)}, u32[]{:S(2)}) copy-start(f32[1,1536]{1,0:T(1,128)} %get-tuple-element.49) | copy-start | bytes 18436
  479.6 17.6 %copy-start.1 = (f32[8,768]{1,0:T(8,128)S(1)}, f32[8,768]{1,0:T(8,128)}, u32[]{:S(2)}) copy-start(f32[8,768]{1,0:T(8,128)} %get-tuple-element.50) | copy-start | bytes 73732
  479.6 18.5 %copy-start = (f32[1,3072]{1,0:T(1,128)S(1)}, f32[1,3072]{1,0:T(1,128)}, u32[]{:S(2)}) copy-start(f32[1,3072]{1,0:T(1,128)} %get-tuple-element.51) | copy-start | bytes 36868
  479.6 19.2 %copy-start.4 = (u32[32]{0:T(128)S(1)}, u32[32]{0:T(128)}, u32[]{:S(2)}) copy-start(u32[32]{0:T(128)} %constant.27) | copy-start | bytes 388
Sparse Core Ops, SparseCore 0:
  194.1 57.5 reduce-scatter.6
  255.6 67.1 reduce-scatter.4
  326.6 74.3 reduce-scatter.8
  404.8 74.7 reduce-scatter.10
  481.9 35.7 all-reduce.11
